TPU v7x, 512 devices: a whole 4x8x8 slice. The times are simulated.
512 devices in a mesh: batch: 32 (over z, x), head: 16 (over y, core).
Axes of the slice: x: 4, y: 8, z: 8, core: 2. Of those that a mesh axis runs over, the one named last changes fastest.
Arguments:
- tokens: bfloat16 [16384, 2048], P('batch', 'head'), may hold values from -96 to 96
- lengths: int32 [128], P('batch'), may hold values from 1 to 128
- states: float32 [128, 16, 128, 128], P('batch', 'head'), may hold values from -3 to 3
- norm_gain: float32 [2048], replicated, may hold values from 0.1 to 1.9
- mix_weight: bfloat16 [2048, 14336], P(None, 'head'), may hold values from -0.125 to 0.125
- rate_weight: bfloat16 [2048, 64], P(None, 'head'), may hold values from -0.5524272 to 0.5524272
- decay_rate: float32 [16], P('head'), may hold values from 0.0005 to 0.03
- head_gain: float32 [128], replicated, may hold values from 0.1 to 1.9
- out_weight: bfloat16 [2048, 2048], P('head'), may hold values from -0.125 to 0.125
- final_gain: float32 [2048], replicated, may hold values from 0.1 to 1.9
- vocab_table: bfloat16 [16384, 2048], P(('batch', 'head')), may hold values from -50.8233 to 50.8233
- next_token: int32 [128], replicated, may hold values from 0 to 16383
Outputs:
- mixed: bfloat16 [16384, 2048], P('batch', 'head')
- new_state: float32 [128, 16, 128, 128], P('batch', 'head')
- log_likelihood: float32 [128], replicated
All inputs are finite; a program needn't handle non-finite values.
Results may differ from a plain program's by a relative error of at most 0.0058.
The roundings to bfloat16 on the way count: a program that leaves them out, or rounds other values in their place, can miss the bound.
Values may be sent and summed in bfloat16 or wider, within the bound.
A program may use at most 64 MiB of HBM per device.

v0:
```python
import jax
import jax.numpy as jnp
from jax import lax
from jax.sharding import Mesh
from jax.sharding import PartitionSpec as P

HEAD_DIM = 128
REFLECT = 3
NEW_POSITIONS = 128
HEAD = ("head_0", "head_1")
BATCH_HEAD = ("batch_0", "batch_1", "head_0", "head_1")
BATCH = ("batch_0", "batch_1")


ROW_EPSILON = 1e-05
KEY_EPSILON = 1e-06
HIGHEST_PRECISION = lax.Precision.HIGHEST


def all_in_one(array, axis):
    leaves = jax.tree.leaves(array)
    order = sorted(range(len(leaves)), key=lambda k: -leaves[k].size)
    width = (1, *leaves[order[0]].shape)[-1]
    lines = [
        jnp.pad(leaves[k].reshape(-1), (0, -leaves[k].size % width)).reshape(-1, width)
        for k in order
    ]
    both, at, found = (lax.all_gather(jnp.concatenate(lines), axis), 0, {})
    for k, line in zip(order, lines):
        share = both[:, at : at + len(line)].reshape(len(both), -1)
        found[k] = share[:, : leaves[k].size].reshape(-1, *leaves[k].shape)
        at += len(line)
    numbers = iter(range(len(leaves)))
    return jax.tree.map(lambda _: found[next(numbers)], array)


def joined_all(array, axes, combine):
    for axis in axes:
        pieces = all_in_one(array, axis)
        array = jax.tree.map(lambda part: part[0], pieces)
        for k in range(1, lax.axis_size(axis)):
            array = combine(array, jax.tree.map(lambda part: part[k], pieces))
    return array


def delta_block(queries, key_rows, value_rows, beta_rows, log_decay, start_state):
    positions = key_rows.shape[0]
    reflections = key_rows.shape[1]
    total_steps = positions * reflections
    flat_keys = key_rows.reshape(total_steps, key_rows.shape[2])
    flat_values = value_rows.reshape(total_steps, value_rows.shape[2])
    flat_betas = beta_rows.reshape(total_steps)
    padding = jnp.zeros((positions, reflections - 1), log_decay.dtype)
    step_decay = jnp.concatenate([log_decay[:, None], padding], axis=1).reshape(total_steps)
    cumulative = jnp.cumsum(step_decay)
    step_index = jnp.arange(total_steps)
    earlier = step_index[:, None] > step_index[None, :]
    decay_ratio = jnp.exp(jnp.where(earlier, cumulative[:, None] - cumulative[None, :], -jnp.inf))
    key_gram = jnp.dot(flat_keys, flat_keys.T, precision=HIGHEST_PRECISION)
    system = (
        jnp.eye(total_steps, dtype=key_gram.dtype) + flat_betas[:, None] * decay_ratio * key_gram
    )
    start_image = jnp.dot(flat_keys, start_state.T, precision=HIGHEST_PRECISION)
    source = flat_betas[:, None] * (flat_values - jnp.exp(cumulative)[:, None] * start_image)
    updates = jax.scipy.linalg.solve_triangular(system, source, lower=True, unit_diagonal=True)
    query_cumulative = cumulative.reshape(positions, reflections)[:, reflections - 1]
    query_step = step_index.reshape(positions, reflections)[:, reflections - 1]
    visible = step_index[None, :] <= query_step[:, None]
    weights = jnp.exp(jnp.where(visible, query_cumulative[:, None] - cumulative[None, :], -jnp.inf))
    scores = jnp.dot(queries, flat_keys.T, precision=HIGHEST_PRECISION) * weights
    attended = jnp.exp(query_cumulative)[:, None] * jnp.dot(
        queries, start_state.T, precision=HIGHEST_PRECISION
    )
    attended = attended + jnp.dot(scores, updates, precision=HIGHEST_PRECISION)
    tail_decay = jnp.exp(cumulative[total_steps - 1] - cumulative)
    new_state = jnp.exp(cumulative[total_steps - 1]) * start_state
    new_state = new_state + jnp.dot(
        updates.T, tail_decay[:, None] * flat_keys, precision=HIGHEST_PRECISION
    )
    return (attended, new_state)


def head_inputs(projected, rate_logits, valid_mask, decay_rate):
    queries = jax.nn.silu(projected[:, :, :, 0])
    key_rows = jax.nn.silu(projected[:, :, :, 1 : REFLECT + 1])
    key_rows = key_rows * lax.rsqrt(
        jnp.sum(key_rows * key_rows, axis=-1, keepdims=True) + KEY_EPSILON
    )
    value_rows = jax.nn.silu(projected[:, :, :, REFLECT + 1 :])
    beta_rows = jnp.where(
        valid_mask[:, :, None, None], 2.0 * jax.nn.sigmoid(rate_logits[..., :REFLECT]), 0.0
    )
    log_decay = jnp.where(
        valid_mask[:, :, None], -decay_rate * jax.nn.softplus(rate_logits[..., REFLECT]), 0.0
    )
    return (queries, key_rows, value_rows, beta_rows, log_decay)


def run_heads(queries, key_rows, value_rows, beta_rows, log_decay, start_states):
    per_head = jax.vmap(delta_block, in_axes=(1, 1, 1, 1, 1, 0), out_axes=(1, 0))
    per_sequence = jax.vmap(per_head)
    return per_sequence(queries, key_rows, value_rows, beta_rows, log_decay, start_states)


def head_norm(attended, head_gain):
    factor = lax.rsqrt(jnp.mean(attended * attended, axis=-1, keepdims=True) + ROW_EPSILON)
    return (attended * factor * head_gain).astype(jnp.bfloat16)


def combine_totals(earlier_part, later_part):
    highest = jnp.maximum(earlier_part[0], later_part[0])
    summed = earlier_part[1] * jnp.exp(earlier_part[0] - highest) + later_part[1] * jnp.exp(
        later_part[0] - highest
    )
    return (highest, summed, earlier_part[2] + later_part[2])


def on_device(
    tokens,
    lengths,
    states,
    norm_gain,
    mix_weight,
    rate_weight,
    decay_rate,
    head_gain,
    out_weight,
    final_gain,
    vocab_table,
    next_token,
):
    sequences = lengths.shape[0]
    local_rows = tokens.shape[0]
    local_width = tokens.shape[1]
    model_width = norm_gain.shape[0]
    local_heads = states.shape[1]
    wide_portion = lax.all_gather(tokens, HEAD, axis=1, tiled=True).astype(jnp.float32)
    scaled = (wide_portion * norm_gain).astype(jnp.bfloat16)
    projected = jnp.dot(scaled, mix_weight, preferred_element_type=jnp.float32)
    rate_logits = jnp.dot(scaled, rate_weight, preferred_element_type=jnp.float32)
    squares = jnp.sum(wide_portion * wide_portion, axis=1)
    projected, rate_logits, squares = (projected, rate_logits, squares)
    inverse = lax.rsqrt(squares / model_width + ROW_EPSILON)
    projected = (projected * inverse[:, None]).reshape(
        sequences, NEW_POSITIONS, local_heads, 2 * REFLECT + 1, HEAD_DIM
    )
    rate_logits = (rate_logits * inverse[:, None]).reshape(
        sequences, NEW_POSITIONS, local_heads, REFLECT + 1
    )
    valid_mask = jnp.arange(NEW_POSITIONS)[None, :] < lengths[:, None]
    queries, key_rows, value_rows, beta_rows, log_decay = head_inputs(
        projected, rate_logits, valid_mask, decay_rate
    )
    attended, new_state = run_heads(queries, key_rows, value_rows, beta_rows, log_decay, states)
    normed = head_norm(attended, head_gain).reshape(local_rows, local_heads * HEAD_DIM)
    columns = lax.all_to_all(out_weight, HEAD, split_axis=1, concat_axis=0, tiled=True)
    mix_sum = jnp.dot(
        lax.all_gather(normed, HEAD, axis=1, tiled=True),
        columns,
        preferred_element_type=jnp.float32,
    )
    mixed = (tokens.astype(jnp.float32) + mix_sum).astype(jnp.bfloat16)
    last_index = (lengths - 1)[:, None, None]
    last_rows = jnp.take_along_axis(
        mixed.reshape(sequences, NEW_POSITIONS, local_width), last_index, axis=1
    )[:, 0]
    gathered = lax.all_gather(last_rows[None], BATCH_HEAD, axis=0, tiled=True)
    batch_count = lax.axis_size(BATCH)
    head_count = lax.axis_size(HEAD)
    everyone = gathered.reshape(batch_count, head_count, sequences, local_width).transpose(
        0, 2, 1, 3
    )
    everyone = everyone.reshape(batch_count * sequences, model_width)
    widened_all = everyone.astype(jnp.float32)
    factor = lax.rsqrt(jnp.mean(widened_all * widened_all, axis=1, keepdims=True) + ROW_EPSILON)
    hidden = (widened_all * factor * final_gain).astype(jnp.bfloat16)
    logits = jnp.dot(hidden, vocab_table.T, preferred_element_type=jnp.float32)
    vocab_here = vocab_table.shape[0]
    vocab_ids = lax.axis_index(BATCH_HEAD) * vocab_here + jnp.arange(vocab_here)
    largest = jnp.max(logits, axis=1)
    exp_total = jnp.sum(jnp.exp(logits - largest[:, None]), axis=1)
    target = jnp.sum(jnp.where(vocab_ids[None, :] == next_token[:, None], logits, 0.0), axis=1)
    largest, exp_total, target = joined_all(
        (largest, exp_total, target), BATCH_HEAD, combine_totals
    )
    return (mixed, new_state, target - (largest + jnp.log(exp_total)))


def solution(mesh):
    torus = Mesh(mesh.devices.reshape(8, 4, 8, 2), ("batch_0", "batch_1", "head_0", "head_1"))
    placed = (
        P(BATCH, HEAD),
        P(BATCH),
        P(BATCH, HEAD, None, None),
        P(),
        P(None, HEAD),
        P(None, HEAD),
        P(HEAD),
        P(),
        P(HEAD, None),
        P(),
        P(BATCH_HEAD, None),
        P(),
    )
    return jax.shard_map(
        on_device,
        mesh=torus,
        in_specs=placed,
        out_specs=(P(BATCH, HEAD), P(BATCH, HEAD, None, None), P()),
        check_vma=False,
    )
```

profile of v0, /device:TPU:1, one launch (start us, length us, event | category | flops | bytes accessed | tf_op | source)
XLA Modules:
  0.0 411.4 jit_solution(3345442622129094462)
XLA Ops:
  9.2 1.1 fusion.28
  10.4 1.2 iota_compare_fusion.5
  13.2 45.9 %all-gather.11.cloned.1.call-done = bf16[512,2048]{1,0:T(8,128)(2,1)} async-done(((bf16[512,128]{1,0:T(8,128)(2,1)}), bf16[512,2048]{1,0:T(8,128)(2,1)}) %all-gather.11.cloned.1.call-update) | async-done | bytes 2097168 | tf_op jit(solution)/shard_map/all_gather | solution.py:137
  59.1 2.1 fusion.1
  61.2 2.4 fusion.19
  64.1 1.2 reduce-window.6
  66.2 5.6 %fusion.6 = f32[512,896]{1,0:T(8,128)} fusion(bf16[2048,896]{1,0:T(8,128)(2,1)} %param.16, bf16[512,2048]{1,0:T(8,128)(2,1)S(1)} %copy-done.1, f32[2048]{0:T(1024)S(1)} %copy-done.21, f32[512]{0:T(512)S(1)} %add_rsqrt_fusion.2), kind=kOutput, calls=%fused_computation.10 | convolution fusion | flops 1882652672 | bytes 7612416 | tf_op jit(solution)/shard_map/dot_general | solution.py:139
  71.8 1.6 reshape.1914
  74.3 1.4 fusion.132
  76.9 1.7 divide_multiply_fusion
  81.3 5.3 %select_add_fusion = f32[4,384,384]{2,1,0:T(8,128)} fusion(f32[384,384]{1,0:T(8,128)} %get-tuple-element.100, f32[4,384]{1,0:T(4,128)S(1)} %get-tuple-element.86, f32[4,384]{1,0:T(4,128)S(1)} %mul.576, f32[384,384]{1,0:T(8,128)} %get-tuple-element.99, pred[384,384]{1,0:T(8,128)(4,1)S(1)} %copy-done.7, pred[384,384]{1,0:T(8,128)(4,1)S(1)} %copy-done.8, ...), kind=kOutput, calls=%fused_computation.7 | convolution fusion | flops 910098432 | bytes 4632576 | tf_op jit(solution)/shard_map/vmap(vmap())/dot_general | solution.py:59
  86.6 11.4 %while.1 = (s32[]{:T(128)}, f32[4,1,384,384]{3,2,1,0:T(8,128)}, s32[3,2]{0,1:T(2,128)S(1)}, f32[3,4,1,128,128]{4,3,0,2,1:T(8,128)}, s32[]{:T(128)}) while((s32[]{:T(128)}, f32[4,1,384,384]{3,2,1,0:T(8,128)}, s32[3,2]{0,1:T(2,128)S(1)}, f32[3,4,1,128,128]{4,3,0,2,1:T(8,128)}, s32[]{:T(128)}) %tuple.58), condition=%wide.while_cond, body=%wide.while_body.sunk | while | flops 2 | bytes 525421 | solution.py:65
  87.2 3.2 bitcast_dynamic-update-slice_fusion.2
  91.0 3.2 bitcast_dynamic-update-slice_fusion.2
  94.9 3.1 bitcast_dynamic-update-slice_fusion.2
  98.0 118.9 %custom-call.4 = f32[4,1,3,128,128]{3,4,2,1,0:T(8,128)S(1)} custom-call(f32[4,1,3,128,128]{4,3,2,1,0:T(8,128)} %bitcast.624), custom_call_target="InvertDiagBlocksLowerTriangular" | custom-call | tf_op jit(solution)/shard_map/vmap(vmap(jit(_solve_triangular)))/triangular_solve | solution.py:65
  216.9 0.9 fusion.11
  218.4 1.4 fusion.13
  220.4 1.7 fusion.15
  223.9 1.1 convolution_multiply_fusion.1
  224.9 1.0 multiply_reduce_fusion.2
  226.8 1.0 copy.235
  227.8 5.1 %all-to-all-start = ((bf16[128,16,128]{0,2,1:T(8,128)(2,1)}), bf16[128,16,128]{0,2,1:T(8,128)(2,1)S(1)}, u32[]{:S(2)}, u32[]{:S(2)}) async-start(bf16[128,16,128]{0,2,1:T(8,128)(2,1)} %bitcast.33), calls=%async_computation | async-start | bytes 1048576 | tf_op jit(solution)/shard_map/all_to_all | solution.py:156
  233.0 18.5 %all-to-all-done = bf16[128,16,128]{0,2,1:T(8,128)(2,1)S(1)} async-done(((bf16[128,16,128]{0,2,1:T(8,128)(2,1)}), bf16[128,16,128]{0,2,1:T(8,128)(2,1)S(1)}, u32[]{:S(2)}, u32[]{:S(2)}) %all-to-all-start) | async-done | bytes 524320 | tf_op jit(solution)/shard_map/all_to_all | solution.py:156
  253.1 2.1 fusion.17
  255.3 18.9 %all-gather.13.cloned.1.call-done = bf16[512,2048]{1,0:T(8,128)(2,1)} async-done(((bf16[512,128]{1,0:T(8,128)(2,1)}), bf16[512,2048]{1,0:T(8,128)(2,1)}) %all-gather.13.cloned.1.call-update) | async-done | bytes 2097168 | tf_op jit(solution)/shard_map/all_gather | solution.py:158
  274.2 2.3 fusion.18
  277.2 70.2 %all_gather.35 = bf16[512,4,128]{2,1,0:T(4,128)(2,1)S(1)} all-gather(bf16[1,4,128]{2,1,0:T(4,128)(2,1)S(1)} %bitcast_select_fusion), channel_id=1, replica_groups=mesh['batch_0'=8,'batch_1'=4,'head_0'=8,'head_1'=2] {'batch_0','batch_1'..., dimensions={0}, use_global_device_ids=true | all-gather | bytes 525312 | tf_op jit(solution)/shard_map/all_gather | solution.py:167
  348.9 15.8 %all-gather.4 = f32[8,3,128]{2,1,0:T(4,128)S(1)} all-gather(f32[1,3,128]{2,1,0:T(4,128)S(1)} %maximum_bitcast_fusion.5), channel_id=2, replica_groups=mesh['batch_0'=8,'batch_1'=4,'head_0'=8,'head_1'=2] {'batch_0'}, dimensions={0}, use_global_device_ids=true | all-gather | bytes 13824 | tf_op jit(solution)/shard_map/all_gather | solution.py:28
  364.8 8.1 %all-gather.5 = f32[4,3,128]{2,1,0:T(4,128)S(1)} all-gather(f32[1,3,128]{2,1,0:T(4,128)S(1)} %maximum_bitcast_fusion.6), channel_id=3, replica_groups=mesh['batch_0'=8,'batch_1'=4,'head_0'=8,'head_1'=2] {'batch_1'}, dimensions={0}, use_global_device_ids=true | all-gather | bytes 7680 | tf_op jit(solution)/shard_map/all_gather | solution.py:28
  373.0 15.6 %all-gather.6 = f32[8,3,128]{2,1,0:T(4,128)S(1)} all-gather(f32[1,3,128]{2,1,0:T(4,128)S(1)} %maximum_bitcast_fusion.7), channel_id=4, replica_groups=mesh['batch_0'=8,'batch_1'=4,'head_0'=8,'head_1'=2] {'head_0'}, dimensions={0}, use_global_device_ids=true | all-gather | bytes 13824 | tf_op jit(solution)/shard_map/all_gather | solution.py:28
  388.6 15.4 %all-gather.7 = f32[2,3,128]{2,1,0:T(4,128)S(1)} all-gather(f32[1,3,128]{2,1,0:T(4,128)S(1)} %maximum_bitcast_fusion.8), channel_id=5, replica_groups=mesh['batch_0'=8,'batch_1'=4,'head_0'=8,'head_1'=2] {'head_1'}, dimensions={0}, use_global_device_ids=true | all-gather | bytes 4608 | tf_op jit(solution)/shard_map/all_gather | solution.py:28
  (131 shorter events, 19.0 us)
Async XLA Ops:
  7.2 341.1 %copy-start = (bf16[32,2048]{1,0:T(8,128)(2,1)S(1)}, bf16[32,2048]{1,0:T(8,128)(2,1)}, u32[]{:S(2)}) copy-start(bf16[32,2048]{1,0:T(8,128)(2,1)} %param.22) | copy-start | bytes 393220
  7.2 54.0 %copy-start.20 = (bf16[2048,4]{0,1:T(4,128)(2,1)S(1)}, bf16[2048,4]{0,1:T(4,128)(2,1)}, u32[]{:S(2)}) copy-start(bf16[2048,4]{0,1:T(4,128)(2,1)} %param.17) | copy-start | bytes 49156
  7.2 54.0 %copy-start.21 = (f32[2048]{0:T(1024)S(1)}, f32[2048]{0:T(1024)}, u32[]{:S(2)}) copy-start(f32[2048]{0:T(1024)} %param.15) | copy-start | bytes 24580
  7.2 51.9 %all-gather.11.cloned.1.call-start = ((), (), s32[]{:S(2)}) async-start(), calls=%async_computation.1 | async-start | bytes 2228224 | tf_op jit(solution)/shard_map/all_gather | solution.py:137
  7.9 266.2 %all-gather.13.cloned.1.call-start = ((), (), s32[]{:S(2)}) async-start(), calls=%async_computation.2 | async-start | bytes 2228224 | tf_op jit(solution)/shard_map/all_gather | solution.py:158
  13.2 50.4 %copy-start.17 = (s32[4]{0:T(128)S(1)}, s32[4]{0:T(128)}, u32[]{:S(2)}) copy-start(s32[4]{0:T(128)} %param.13) | copy-start | bytes 52
  61.2 5.0 %copy-start.1 = (bf16[512,2048]{1,0:T(8,128)(2,1)S(1)}, bf16[512,2048]{1,0:T(8,128)(2,1)}, u32[]{:S(2)}) copy-start(bf16[512,2048]{1,0:T(8,128)(2,1)} %all-gather.11.cloned.1.call-done) | copy-start | bytes 6291460
  63.6 13.0 %copy-start.10 = (f32[4,128,1,4]{1,0,3,2:T(4,128)}, f32[4,128,1,4]{1,0,3,2:T(4,128)S(1)}, u32[]{:S(2)}) copy-start(f32[4,128,1,4]{1,0,3,2:T(4,128)S(1)} %reshape.1828) | copy-start | bytes 24580
  78.6 0.9 slice-start
  78.6 1.1 copy-start.16
  78.9 2.4 copy-start.7
  78.9 2.3 copy-start.8
  80.7 0.5 copy-start.14
  81.2 5.3 %copy-start.11 = (f32[4,384]{1,0:T(4,128)}, f32[4,384]{1,0:T(4,128)S(1)}, u32[]{:S(2)}) copy-start(f32[4,384]{1,0:T(4,128)S(1)} %get-tuple-element.86) | copy-start | bytes 18436
  81.3 5.3 %copy-start.22 = (s32[3]{0:T(128)S(1)}, s32[3]{0:T(128)}, u32[]{:S(2)}) copy-start(s32[3]{0:T(128)} %iota_multiply_fusion) | copy-start | bytes 40
  86.6 130.3 %copy-start.2 = (f32[4,1,128,128]{3,2,1,0:T(8,128)S(1)}, f32[4,1,128,128]{3,2,1,0:T(8,128)}, u32[]{:S(2)}) copy-start(f32[4,1,128,128]{3,2,1,0:T(8,128)} %param.14) | copy-start | bytes 786436
  218.4 4.7 %copy-start.5 = (f32[4,128,1,1,128]{4,3,1,0,2:T(1,128)S(1)}, f32[4,128,1,1,128]{4,3,1,0,2:T(1,128)}, u32[]{:S(2)}) copy-start(f32[4,128,1,1,128]{4,3,1,0,2:T(1,128)} %slice.495) | copy-start | bytes 786436
  219.8 4.0 copy-start.9
  219.8 4.0 copy-start.12
  223.8 2.1 copy-start.15
  223.8 2.9 copy-start.4
  225.9 7.0 %copy-start.18 = (s32[4]{0:T(128)S(1)}, s32[4]{0:T(128)}, u32[]{:S(2)}) copy-start(s32[4]{0:T(128)} %param.13) | copy-start | bytes 52
  227.8 23.8 %all-to-all-start = ((bf16[128,16,128]{0,2,1:T(8,128)(2,1)}), bf16[128,16,128]{0,2,1:T(8,128)(2,1)S(1)}, u32[]{:S(2)}, u32[]{:S(2)}) async-start(bf16[128,16,128]{0,2,1:T(8,128)(2,1)} %bitcast.33), calls=%async_computation | async-start | bytes 1048576 | tf_op jit(solution)/shard_map/all_to_all | solution.py:156
  251.5 22.6 %copy-start.3 = (bf16[512,128]{1,0:T(8,128)(2,1)S(1)}, bf16[512,128]{1,0:T(8,128)(2,1)}, u32[]{:S(2)}) copy-start(bf16[512,128]{1,0:T(8,128)(2,1)} %param.12) | copy-start | bytes 393220
  274.2 74.1 %copy-start.13 = (f32[2048]{0:T(1024)S(1)}, f32[2048]{0:T(1024)}, u32[]{:S(2)}) copy-start(f32[2048]{0:T(1024)} %param.21) | copy-start | bytes 24580
  276.5 128.1 %copy-start.6 = (bf16[512,128]{1,0:T(8,128)(2,1)}, bf16[512,128]{1,0:T(8,128)(2,1)S(1)}, u32[]{:S(2)}) copy-start(bf16[512,128]{1,0:T(8,128)(2,1)S(1)} %fusion.18) | copy-start | bytes 393220
  276.5 72.3 %copy-start.19 = (s32[128]{0:T(128)S(1)}, s32[128]{0:T(128)}, u32[]{:S(2)}) copy-start(s32[128]{0:T(128)} %param.23) | copy-start | bytes 1540
Sparse Core Ops, SparseCore 0:
  10.1 48.9 all-gather.10
  226.9 47.2 all-gather.12
where the time goes:
time: 412 us; the launch traced here: 411 us
  other arithmetic  132 us (32%)
  blocking collectives  125 us (30%)
  waiting for transfers between devices  84 us (20%)
  matrix products  26.7 us (6%)
  local copies, waits for them, and re-layouts  22.6 us (5%)
  between operations  15.3 us (4%)
  starting transfers between devices  5.22 us (1%)
    another operation x3, other arithmetic, delta_block(): jax.scipy.linalg.solve_triangular(system, source, lower=True, unit_diagon...  119 us
    all_gather x1, blocking collectives, on_device(): gathered = lax.all_gather(last_rows[None], BATCH_HEAD, axis=0, tiled=True)  70.2 us
    all_gather x4, blocking collectives, all_in_one(): both, at, found = (lax.all_gather(jnp.concatenate(lines), axis), 0, {})  55 us
    all_gather x1, waiting for transfers between devices, on_device(): lax.all_gather(tokens, HEAD, axis=1, tiled=True).astype(jnp.float32)  45.9 us
    all_gather x1, waiting for transfers between devices, on_device(): lax.all_gather(normed, HEAD, axis=1, tiled=True)  18.9 us
    all_to_all x1, waiting for transfers between devices, on_device(): lax.all_to_all(out_weight, HEAD, split_axis=1, concat_axis=0, tiled=True)  18.5 us
    another operation x20, local copies, waits for them, and re-layouts  13.7 us
  transfers between devices with their start and end apart: 3, of which 3 were waited for; matrix products, arithmetic and copies ran while one was open for 2% of the time, Pallas kernels for 0%

commit v1 on v0

v1 whole, which is shorter than its diff:
```python
import jax
import jax.numpy as jnp
from jax import lax
from jax.experimental import pallas as pl
from jax.experimental.pallas import tpu as pltpu
from jax.sharding import Mesh
from jax.sharding import PartitionSpec as P

HEAD_DIM = 128
REFLECT = 3
NEW_POSITIONS = 128
HEAD = ("head_0", "head_1")
BATCH_HEAD = ("batch_0", "batch_1", "head_0", "head_1")
BATCH = ("batch_0", "batch_1")
BF = jnp.bfloat16
F32 = jnp.float32
HI = lax.Precision.HIGHEST
N = 128
CH = 32
NC = N // CH
LEVELS = 7
ROW_EPSILON = 1e-05
KEY_EPSILON = 1e-06


def split(x):
    high = x.astype(BF)
    return high, (x - high.astype(F32)).astype(BF)


def left_of(x):
    high, low = split(x)
    return jnp.concatenate([high, low], axis=1)


def right_of(x):
    high, low = split(x)
    both = jnp.concatenate([high, low], axis=1)
    return jnp.concatenate([both, both], axis=0)


def halves(product):
    return product[:, :N] + product[:, N:]


def dot(a, b):
    return jnp.dot(a, b, preferred_element_type=F32)


def dot_nt(a, b):
    return lax.dot_general(a, b, (((1,), (1,)), ((), ())), preferred_element_type=F32)


def fill_tables(masks, tri, picks):
    row = lax.broadcasted_iota(jnp.int32, (N, N), 0)
    col = lax.broadcasted_iota(jnp.int32, (N, N), 1)
    j, p, jj, pp = row // CH, row % CH, col // CH, col % CH
    steps = (j < 3) & (jj < 3)
    sets = [steps & (p == pp) & (j == 1) & (jj == 0), steps & (p == pp) & (j == 2) & (jj < 2)]
    for k in range(5):
        same = (p >> (k + 1)) == (pp >> (k + 1))
        sets.append(steps & same & (((p >> k) & 1) == 1) & (((pp >> k) & 1) == 0))
    sets.append((j == 3) & (jj < 3))
    for k, chosen in enumerate(sets):
        masks[k] = chosen.astype(F32)
    strict = steps & ((p > pp) | ((p == pp) & (j > jj)))
    masks[LEVELS + 1] = (strict | ((j == 3) & (jj < 3) & (p >= pp))).astype(F32)
    tri[...] = ((j == jj) & (pp <= p)).astype(F32)
    for c in range(NC):
        picks[:, c * N : (c + 1) * N] = ((j == c) & (p <= pp)).astype(F32)


def silu(v):
    return v / (1.0 + jnp.exp(-v))


def softplus(v):
    return jnp.maximum(v, 0.0) + jnp.log1p(jnp.exp(-jnp.abs(v)))


def sequence_inputs(s, length, rate, blocks, gain, weight, rate_t, masks, tri, picks, xs, la, tt, xh, xl, kt, eq, et):
    count = blocks.shape[0]
    rows = pl.ds(pl.multiple_of(s * N, N), N)
    squares = jnp.zeros((N, N), F32)
    for b in range(count):
        wide = blocks[b, rows, :].astype(F32)
        squares = squares + wide * wide
        xs[:, b * N : (b + 1) * N] = (wide * gain[b : b + 1, :]).astype(BF)
    inverse = lax.rsqrt(jnp.sum(squares, axis=1, keepdims=True) / (count * N) + ROW_EPSILON)
    projected = dot(xs[...], weight[...]) * inverse
    rates = dot_nt(xs[...], rate_t[...]) * inverse
    query = silu(projected[:, :N])
    keys, values = [], []
    for j in range(3):
        key = silu(projected[:, (1 + j) * N : (2 + j) * N])
        keys.append(key * lax.rsqrt(jnp.sum(key * key, axis=1, keepdims=True) + KEY_EPSILON))
        values.append(silu(projected[:, (4 + j) * N : (5 + j) * N]))
    valid = lax.broadcasted_iota(jnp.int32, (N, 1), 0) < length
    betas = [
        jnp.broadcast_to(jnp.where(valid, 2.0 * jax.nn.sigmoid(rates[:, j : j + 1]), 0.0), (N, N))
        for j in range(3)
    ]
    decay = jnp.where(valid, -rate * softplus(rates[:, 3:4]), 0.0)
    decay = jnp.broadcast_to(decay, (N, N))
    cum = jnp.dot(tri[...], decay, precision=HI, preferred_element_type=F32)
    cum_row = jnp.dot(decay.T[:8], picks[...], precision=HI, preferred_element_type=F32)
    grow = jnp.exp(cum)
    one = jnp.ones((CH, N), F32)
    zero = jnp.zeros((CH, N), F32)
    eye = (
        lax.broadcasted_iota(jnp.int32, (N, N), 0) == lax.broadcasted_iota(jnp.int32, (N, N), 1)
    ).astype(F32)
    causal = masks[LEVELS + 1] > 0.5
    first = masks[0]
    for c in range(NC):
        at = slice(c * CH, (c + 1) * CH)
        n = s * NC + c
        kq = jnp.concatenate([keys[0][at], keys[1][at], keys[2][at], query[at]], axis=0)
        vv = jnp.concatenate([values[0][at], values[1][at], values[2][at], zero], axis=0)
        bb = jnp.concatenate([betas[0][at], betas[1][at], betas[2][at], one], axis=0)
        cc = jnp.concatenate([cum[at]] * 4, axis=0)
        gg = jnp.concatenate([grow[at]] * 3 + [zero], axis=0)
        high, low = split(kq)
        gram = halves(
            dot_nt(
                jnp.concatenate([high, low], axis=1),
                jnp.concatenate(
                    [jnp.concatenate([high, high], axis=1), jnp.concatenate([low, low], axis=1)],
                    axis=0,
                ),
            )
        )
        ratio = jnp.exp(jnp.where(causal, cc - cum_row[0:1, c * N : (c + 1) * N], -1e30))
        system = bb * ratio * gram
        la[n] = system
        tt[n] = eye - system * first
        xa, xb = bb * vv, bb * gg * kq
        ha, lo_a = split(xa)
        hb, lo_b = split(xb)
        xh[n] = jnp.concatenate([ha, hb], axis=1)
        xl[n] = jnp.concatenate([lo_a, lo_b], axis=1)
        last = cum[(c + 1) * CH - 1 : (c + 1) * CH, :]
        tail = jnp.concatenate([jnp.exp(last - cum[at])] * 3 + [zero], axis=0)
        kt[n] = left_of((tail * kq).T)
        eq[n] = grow[at] * query[at]
        et[n] = jnp.broadcast_to(jnp.exp(last), (8, N))


def invert(ids, masks, la, tt, tmp):
    def level(k, carry):
        mask = masks[k]
        for n in ids:
            tmp[n] = halves(dot(left_of(la[n] * mask), right_of(tt[n])))
        for n in ids:
            t = tt[n]
            tt[n] = t - halves(dot(left_of(t), right_of(tmp[n])))
        return carry

    lax.fori_loop(1, LEVELS + 1, level, 0)


def chunk_maps(n, tt, xh, xl, kt, eq, et, pq, rr, ov):
    high, low = split(tt[n])
    big = jnp.concatenate([high, low], axis=1)
    z = dot(big, jnp.concatenate([xh[n], xh[n]], axis=0)) + dot(high, xl[n])
    zh, zl = split(z)
    k = kt[n]
    maps = dot(k, jnp.concatenate([zh, zh], axis=0)) + dot(k[:, :N], zl)
    eye = (
        lax.broadcasted_iota(jnp.int32, (N, N), 0) == lax.broadcasted_iota(jnp.int32, (N, N), 1)
    ).astype(F32)
    p = eye * et[n, 0:1, :] - maps[:, N:]
    pq[n] = left_of(jnp.concatenate([p, eq[n] + z[3 * CH :, N:]], axis=0))
    rr[n] = maps[:, :N]
    ov[n] = -z[3 * CH :, :N]


def run_chain(sequences, states, new_state, normed, head_gain, pq, rr, ov):
    carried = [states[s].T for s in sequences]
    for c in range(NC):
        for k, s in enumerate(sequences):
            n = s * NC + c
            both = halves(dot(pq[n], right_of(carried[k])))
            carried[k] = both[:N] + rr[n]
            attended = both[N:] + ov[n]
            factor = lax.rsqrt(jnp.mean(attended * attended, axis=1, keepdims=True) + ROW_EPSILON)
            normed[s * N + c * CH : s * N + (c + 1) * CH, :] = (
                attended * factor * head_gain[...]
            ).astype(BF)
    for k, s in enumerate(sequences):
        new_state[s] = carried[k].T


def mixer_scratch(seqs, count, width):
    m = seqs * NC
    return [
        pltpu.VMEM((LEVELS + 2, N, N), F32),
        pltpu.VMEM((N, N), F32),
        pltpu.VMEM((N, NC * N), F32),
        pltpu.VMEM((N, count * N), BF),
        pltpu.VMEM((m, N, N), F32),
        pltpu.VMEM((m, N, N), F32),
        pltpu.VMEM((m, N, N), F32),
        pltpu.VMEM((m, N, 2 * N), BF),
        pltpu.VMEM((m, N, 2 * N), BF),
        pltpu.VMEM((m, N, 2 * N), BF),
        pltpu.VMEM((m, CH, N), F32),
        pltpu.VMEM((m, 8, N), F32),
        pltpu.VMEM((m, N + CH, 2 * N), BF),
        pltpu.VMEM((m, N, N), F32),
        pltpu.VMEM((m, CH, N), F32),
    ]


def mixer_kernel(lengths, rate, blocks, gain, weight, rate_t, head_gain, states, normed, new_state, masks, tri, picks, xs, la, tt, tmp, xh, xl, kt, eq, et, pq, rr, ov):
    seqs = states.shape[0]
    fill_tables(masks, tri, picks)

    def one(s, carry):
        sequence_inputs(s, lengths[s], rate[0], blocks, gain, weight, rate_t, masks, tri, picks, xs, la, tt, xh, xl, kt, eq, et)
        return carry

    lax.fori_loop(0, seqs, one, 0)
    invert(range(seqs * NC), masks, la, tt, tmp)

    def maps(s, carry):
        for c in range(NC):
            chunk_maps(s * NC + c, tt, xh, xl, kt, eq, et, pq, rr, ov)
        return carry

    lax.fori_loop(0, seqs, maps, 0)
    run_chain(range(seqs), states, new_state, normed, head_gain, pq, rr, ov)


def mixer(lengths, rate, blocks, gain, weight, rate_t, head_gain, states):
    seqs, rows, count = states.shape[0], blocks.shape[1], blocks.shape[0]
    vmem = pl.BlockSpec(memory_space=pltpu.VMEM)
    smem = pl.BlockSpec(memory_space=pltpu.SMEM)
    return pl.pallas_call(
        mixer_kernel,
        out_shape=(
            jax.ShapeDtypeStruct((rows, N), BF),
            jax.ShapeDtypeStruct((seqs, N, N), F32),
        ),
        in_specs=[smem, smem] + [vmem] * 6,
        out_specs=(vmem, vmem),
        scratch_shapes=mixer_scratch(seqs, count, weight.shape[1]),
        compiler_params=pltpu.CompilerParams(vmem_limit_bytes=56 * 1024 * 1024),
    )(lengths, rate, blocks, gain, weight, rate_t, head_gain, states)


def all_in_one(array, axis):
    leaves = jax.tree.leaves(array)
    order = sorted(range(len(leaves)), key=lambda k: -leaves[k].size)
    width = (1, *leaves[order[0]].shape)[-1]
    lines = [
        jnp.pad(leaves[k].reshape(-1), (0, -leaves[k].size % width)).reshape(-1, width)
        for k in order
    ]
    both, at, found = (lax.all_gather(jnp.concatenate(lines), axis), 0, {})
    for k, line in zip(order, lines):
        share = both[:, at : at + len(line)].reshape(len(both), -1)
        found[k] = share[:, : leaves[k].size].reshape(-1, *leaves[k].shape)
        at += len(line)
    numbers = iter(range(len(leaves)))
    return jax.tree.map(lambda _: found[next(numbers)], array)


def joined_all(array, axes, combine):
    for axis in axes:
        pieces = all_in_one(array, axis)
        array = jax.tree.map(lambda part: part[0], pieces)
        for k in range(1, lax.axis_size(axis)):
            array = combine(array, jax.tree.map(lambda part: part[k], pieces))
    return array


def combine_totals(earlier_part, later_part):
    highest = jnp.maximum(earlier_part[0], later_part[0])
    summed = earlier_part[1] * jnp.exp(earlier_part[0] - highest) + later_part[1] * jnp.exp(
        later_part[0] - highest
    )
    return (highest, summed, earlier_part[2] + later_part[2])


def on_device(
    tokens,
    lengths,
    states,
    norm_gain,
    mix_weight,
    rate_weight,
    decay_rate,
    head_gain,
    out_weight,
    final_gain,
    vocab_table,
    next_token,
):
    sequences = lengths.shape[0]
    local_width = tokens.shape[1]
    model_width = norm_gain.shape[0]
    blocks = lax.all_gather(tokens, HEAD, axis=0)
    normed, new_state = mixer(
        lengths,
        decay_rate,
        blocks,
        norm_gain.reshape(-1, N),
        mix_weight,
        rate_weight.T,
        head_gain.reshape(1, N),
        states[:, 0],
    )
    new_state = new_state[:, None]
    columns = lax.all_to_all(out_weight, HEAD, split_axis=1, concat_axis=0, tiled=True)
    mix_sum = jnp.dot(
        lax.all_gather(normed, HEAD, axis=1, tiled=True),
        columns,
        preferred_element_type=jnp.float32,
    )
    mixed = (tokens.astype(jnp.float32) + mix_sum).astype(jnp.bfloat16)
    last_index = (lengths - 1)[:, None, None]
    last_rows = jnp.take_along_axis(
        mixed.reshape(sequences, NEW_POSITIONS, local_width), last_index, axis=1
    )[:, 0]
    gathered = lax.all_gather(last_rows[None], BATCH_HEAD, axis=0, tiled=True)
    batch_count = lax.axis_size(BATCH)
    head_count = lax.axis_size(HEAD)
    everyone = gathered.reshape(batch_count, head_count, sequences, local_width).transpose(
        0, 2, 1, 3
    )
    everyone = everyone.reshape(batch_count * sequences, model_width)
    widened_all = everyone.astype(jnp.float32)
    factor = lax.rsqrt(jnp.mean(widened_all * widened_all, axis=1, keepdims=True) + ROW_EPSILON)
    hidden = (widened_all * factor * final_gain).astype(jnp.bfloat16)
    logits = jnp.dot(hidden, vocab_table.T, preferred_element_type=jnp.float32)
    vocab_here = vocab_table.shape[0]
    vocab_ids = lax.axis_index(BATCH_HEAD) * vocab_here + jnp.arange(vocab_here)
    largest = jnp.max(logits, axis=1)
    exp_total = jnp.sum(jnp.exp(logits - largest[:, None]), axis=1)
    target = jnp.sum(jnp.where(vocab_ids[None, :] == next_token[:, None], logits, 0.0), axis=1)
    largest, exp_total, target = joined_all(
        (largest, exp_total, target), BATCH_HEAD, combine_totals
    )
    return (mixed, new_state, target - (largest + jnp.log(exp_total)))


def solution(mesh):
    torus = Mesh(mesh.devices.reshape(8, 4, 8, 2), ("batch_0", "batch_1", "head_0", "head_1"))
    placed = (
        P(BATCH, HEAD),
        P(BATCH),
        P(BATCH, HEAD, None, None),
        P(),
        P(None, HEAD),
        P(None, HEAD),
        P(HEAD),
        P(),
        P(HEAD, None),
        P(),
        P(BATCH_HEAD, None),
        P(),
    )
    return jax.shard_map(
        on_device,
        mesh=torus,
        in_specs=placed,
        out_specs=(P(BATCH, HEAD), P(BATCH, HEAD, None, None), P()),
        check_vma=False,
    )
```

time: 412 us -> 262 us (0.64)
  other arithmetic: 132 us -> 1.54 us
  matrix products: 26.7 us -> 2.77 us
  local copies, waits for them, and re-layouts: 22.6 us -> 2.13 us
  Pallas kernels: 0 us -> 19.6 us
  waiting for transfers between devices: 84 us -> 90.3 us
    another operation x5 -> x0, other arithmetic: 121 us -> none  [the longest x3 119 us: delta_block(): jax.scipy.linalg.solve_triangular(system, source, lower=True, unit_diagon...]
    pallas_call x0 -> x1, Pallas kernels: none -> 19.6 us  [mixer(): pl.pallas_call(mixer_kernel, out_shape=(jax.ShapeDtypeStruct((rows, N), B...]
    dot_general x8 -> x0, matrix products: 19 us -> none  [the longest x1 5.61 us: on_device(): projected = jnp.dot(scaled, mix_weight, preferred_element_type=jnp.float32)]
    another operation x21 -> x0, local copies, waits for them, and re-layouts: 13.7 us -> none
    another operation x5 -> x0, matrix products: 4.87 us -> none  [delta_block(): jax.scipy.linalg.solve_triangular(system, source, lower=True, unit_diagon...]
  transfers between devices with their start and end apart: 3 -> 3, of which waited for: 3 -> 3; matrix products, arithmetic and copies ran while one was open for 2% -> 1% of each run, Pallas kernels for 0% -> 0%
where the time goes in v1:
time: 262 us
  blocking collectives  126 us (48%)
  waiting for transfers between devices  90.3 us (34%)
  Pallas kernels  19.6 us (7%)
  between operations  14.9 us (6%)
  starting transfers between devices  4.94 us (2%)
  matrix products  2.77 us (1%)
    all_gather x1, blocking collectives, on_device(): gathered = lax.all_gather(last_rows[None], BATCH_HEAD, axis=0, tiled=True)  70.3 us
    all_gather x4, blocking collectives, all_in_one(): both, at, found = (lax.all_gather(jnp.concatenate(lines), axis), 0, {})  55.3 us
    all_gather x1, waiting for transfers between devices, on_device(): blocks = lax.all_gather(tokens, HEAD, axis=0)  49.2 us
    all_gather x1, waiting for transfers between devices, on_device(): lax.all_gather(normed, HEAD, axis=1, tiled=True)  21.9 us
    pallas_call x1, Pallas kernels, mixer(): pl.pallas_call(mixer_kernel, out_shape=(jax.ShapeDtypeStruct((rows, N), B...  19.6 us
    all_to_all x1, waiting for transfers between devices, on_device(): lax.all_to_all(out_weight, HEAD, split_axis=1, concat_axis=0, tiled=True)  18.5 us
  transfers between devices with their start and end apart: 3, of which 3 were waited for; matrix products, arithmetic and copies ran while one was open for 1% of the time, Pallas kernels for 0%

profile of v1, /device:TPU:1, one launch (start us, length us, event | category | flops | bytes accessed | tf_op | source)
XLA Modules:
  0.0 261.7 jit_solution(153283828679413667)
XLA Ops:
  7.2 0.0 copy-start
  7.2 0.0 all-gather.14.cloned.1.call-start
  7.2 0.7 all-gather.14.cloned.1.call-update
  7.9 0.0 all-gather.12.cloned.1.call-start
  8.6 49.2 %all-gather.14.cloned.1.call-done = bf16[8192,128]{1,0:T(8,128)(2,1)} async-done(((bf16[512,128]{1,0:T(8,128)(2,1)}), bf16[8192,128]{1,0:T(8,128)(2,1)}) %all-gather.14.cloned.1.call-update) | async-done | bytes 2097168 | tf_op jit(solution)/shard_map/all_gather | solution.py:303
  57.8 19.6 %shard_map.139 = (bf16[512,128]{1,0:T(8,128)(2,1)}, f32[4,128,128]{2,1,0:T(8,128)}) custom-call(s32[4]{0:T(128)} %lengths.1, f32[1]{0:T(128)S(6)} %copy.53.rate, bf16[16,512,128]{2,1,0:T(8,128)(2,1)} %bitcast.472, f32[16,128]{1,0:T(8,128)} %bitcast.476, bf16[2048,896]{1,0:T(8,128)(2,1)} %weight.1, bf16[4,2048]{1,0:T(4,128)(2,1)} %bitcast.475, ...), custom_call_target="tpu_custom_call" | custom-call | tf_op jit(solution)/shard_map/pallas_call | solution.py:239
  77.4 0.0 all-gather.12.cloned.1.call-update
  77.4 0.0 copy-done.2
  77.4 1.0 copy.37
  78.4 4.9 %all-to-all-start = ((bf16[128,16,128]{0,2,1:T(8,128)(2,1)}), bf16[128,16,128]{0,2,1:T(8,128)(2,1)S(1)}, u32[]{:S(2)}, u32[]{:S(2)}) async-start(bf16[128,16,128]{0,2,1:T(8,128)(2,1)} %bitcast.5), calls=%async_computation | async-start | bytes 1048576 | tf_op jit(solution)/shard_map/all_to_all | solution.py:315
  83.3 0.0 copy-done.6
  83.4 18.5 %all-to-all-done = bf16[128,16,128]{0,2,1:T(8,128)(2,1)S(1)} async-done(((bf16[128,16,128]{0,2,1:T(8,128)(2,1)}), bf16[128,16,128]{0,2,1:T(8,128)(2,1)S(1)}, u32[]{:S(2)}, u32[]{:S(2)}) %all-to-all-start) | async-done | bytes 524320 | tf_op jit(solution)/shard_map/all_to_all | solution.py:315
  101.9 0.3 copy.38
  102.2 21.9 %all-gather.12.cloned.1.call-done = bf16[512,2048]{1,0:T(8,128)(2,1)} async-done(((bf16[512,128]{1,0:T(8,128)(2,1)}), bf16[512,2048]{1,0:T(8,128)(2,1)}) %all-gather.12.cloned.1.call-update) | async-done | bytes 2097168 | tf_op jit(solution)/shard_map/all_gather | solution.py:317
  124.1 0.0 copy-done.1
  124.1 2.3 fusion
  126.4 0.0 copy-start.3
  126.4 0.0 copy-start.4
  126.4 0.6 gather_fusion
  127.0 0.1 bitcast_select_fusion
  127.1 70.3 %all_gather.39 = bf16[512,4,128]{2,1,0:T(4,128)(2,1)S(1)} all-gather(bf16[1,4,128]{2,1,0:T(4,128)(2,1)S(1)} %bitcast_select_fusion), channel_id=1, replica_groups=mesh['batch_0'=8,'batch_1'=4,'head_0'=8,'head_1'=2] {'batch_0','batch_1'..., dimensions={0}, use_global_device_ids=true | all-gather | bytes 525312 | tf_op jit(solution)/shard_map/all_gather | solution.py:326
  197.4 0.6 multiply_reduce_fusion
  198.0 0.1 copy.39
  198.2 0.1 rsqrt.12
  198.3 0.0 copy-done
  198.3 0.5 fusion.86
  198.8 0.1 exponential_reduce_fusion
  198.9 15.7 %all-gather.5 = f32[8,3,128]{2,1,0:T(4,128)S(1)} all-gather(f32[1,3,128]{2,1,0:T(4,128)S(1)} %maximum_bitcast_fusion), channel_id=3, replica_groups=mesh['batch_0'=8,'batch_1'=4,'head_0'=8,'head_1'=2] {'batch_0'}, dimensions={0}, use_global_device_ids=true | all-gather | bytes 13824 | tf_op jit(solution)/shard_map/all_gather | solution.py:260
  214.7 8.1 %all-gather.6 = f32[4,3,128]{2,1,0:T(4,128)S(1)} all-gather(f32[1,3,128]{2,1,0:T(4,128)S(1)} %maximum_bitcast_fusion.1), channel_id=4, replica_groups=mesh['batch_0'=8,'batch_1'=4,'head_0'=8,'head_1'=2] {'batch_1'}, dimensions={0}, use_global_device_ids=true | all-gather | bytes 7680 | tf_op jit(solution)/shard_map/all_gather | solution.py:260
  222.8 15.9 %all-gather.7 = f32[8,3,128]{2,1,0:T(4,128)S(1)} all-gather(f32[1,3,128]{2,1,0:T(4,128)S(1)} %maximum_bitcast_fusion.2), channel_id=5, replica_groups=mesh['batch_0'=8,'batch_1'=4,'head_0'=8,'head_1'=2] {'head_0'}, dimensions={0}, use_global_device_ids=true | all-gather | bytes 13824 | tf_op jit(solution)/shard_map/all_gather | solution.py:260
  238.9 15.5 %all-gather.8 = f32[2,3,128]{2,1,0:T(4,128)S(1)} all-gather(f32[1,3,128]{2,1,0:T(4,128)S(1)} %maximum_bitcast_fusion.3), channel_id=6, replica_groups=mesh['batch_0'=8,'batch_1'=4,'head_0'=8,'head_1'=2] {'head_1'}, dimensions={0}, use_global_device_ids=true | all-gather | bytes 4608 | tf_op jit(solution)/shard_map/all_gather | solution.py:260
  254.4 0.5 fusion.9
  (25 shorter events, 0.3 us)
Async XLA Ops:
  7.2 191.1 %copy-start = (bf16[32,2048]{1,0:T(8,128)(2,1)S(1)}, bf16[32,2048]{1,0:T(8,128)(2,1)}, u32[]{:S(2)}) copy-start(bf16[32,2048]{1,0:T(8,128)(2,1)} %param.22) | copy-start | bytes 393220
  7.2 50.6 %all-gather.14.cloned.1.call-start = ((), (), s32[]{:S(2)}) async-start(), calls=%async_computation.2 | async-start | bytes 2228224 | tf_op jit(solution)/shard_map/all_gather | solution.py:303
  7.9 116.1 %all-gather.12.cloned.1.call-start = ((), (), s32[]{:S(2)}) async-start(), calls=%async_computation.1 | async-start | bytes 2228224 | tf_op jit(solution)/shard_map/all_gather | solution.py:317
  57.8 19.6 %copy-start.2 = (bf16[128,2048]{1,0:T(8,128)(2,1)S(1)}, bf16[128,2048]{1,0:T(8,128)(2,1)}, u32[]{:S(2)}) copy-start(bf16[128,2048]{1,0:T(8,128)(2,1)} %param.20) | copy-start | bytes 1572868
  77.4 5.9 %copy-start.6 = (s32[4]{0:T(128)S(1)}, s32[4]{0:T(128)}, u32[]{:S(2)}) copy-start(s32[4]{0:T(128)} %lengths.1) | copy-start | bytes 52
  77.4 46.7 %copy-start.1 = (bf16[512,128]{1,0:T(8,128)(2,1)S(1)}, bf16[512,128]{1,0:T(8,128)(2,1)}, u32[]{:S(2)}) copy-start(bf16[512,128]{1,0:T(8,128)(2,1)} %param.12) | copy-start | bytes 393220
  78.4 23.5 %all-to-all-start = ((bf16[128,16,128]{0,2,1:T(8,128)(2,1)}), bf16[128,16,128]{0,2,1:T(8,128)(2,1)S(1)}, u32[]{:S(2)}, u32[]{:S(2)}) async-start(bf16[128,16,128]{0,2,1:T(8,128)(2,1)} %bitcast.5), calls=%async_computation | async-start | bytes 1048576 | tf_op jit(solution)/shard_map/all_to_all | solution.py:315
  126.4 72.4 %copy-start.3 = (bf16[512,128]{1,0:T(8,128)(2,1)}, bf16[512,128]{1,0:T(8,128)(2,1)S(1)}, u32[]{:S(2)}) copy-start(bf16[512,128]{1,0:T(8,128)(2,1)S(1)} %fusion) | copy-start | bytes 393220
  126.4 71.9 %copy-start.4 = (f32[2048]{0:T(1024)S(1)}, f32[2048]{0:T(1024)}, u32[]{:S(2)}) copy-start(f32[2048]{0:T(1024)} %param.21) | copy-start | bytes 24580
  127.0 71.7 %copy-start.5 = (s32[128]{0:T(128)S(1)}, s32[128]{0:T(128)}, u32[]{:S(2)}) copy-start(s32[128]{0:T(128)} %param.23) | copy-start | bytes 1540
Sparse Core Ops, SparseCore 0:
  10.1 47.6 all-gather.13
  77.5 46.4 all-gather.11

commit v2 on v1

v2 whole, which is shorter than its diff:
```python
import functools
import jax
import jax.numpy as jnp
from jax import lax
from jax.experimental import pallas as pl
from jax.experimental.pallas import tpu as pltpu
from jax.sharding import Mesh
from jax.sharding import PartitionSpec as P

BF = jnp.bfloat16
F32 = jnp.float32
HI = lax.Precision.HIGHEST
N = 128
CH = 32
NC = N // CH
LEVELS = 7
ROW_EPSILON = 1e-05
KEY_EPSILON = 1e-06


def split(x):
    high = x.astype(BF)
    return high, (x - high.astype(F32)).astype(BF)


def left_of(x):
    high, low = split(x)
    return jnp.concatenate([high, low], axis=1)


def right_of(x):
    high, low = split(x)
    both = jnp.concatenate([high, low], axis=1)
    return jnp.concatenate([both, both], axis=0)


def halves(product):
    return product[:, :N] + product[:, N:]


def dot(a, b):
    return jnp.dot(a, b, preferred_element_type=F32)


def dot_nt(a, b):
    return lax.dot_general(a, b, (((1,), (1,)), ((), ())), preferred_element_type=F32)


def fill_tables(masks, tri, picks):
    row = lax.broadcasted_iota(jnp.int32, (N, N), 0)
    col = lax.broadcasted_iota(jnp.int32, (N, N), 1)
    j, p, jj, pp = row // CH, row % CH, col // CH, col % CH
    steps = (j < 3) & (jj < 3)
    sets = [steps & (p == pp) & (j == 1) & (jj == 0), steps & (p == pp) & (j == 2) & (jj < 2)]
    for k in range(5):
        same = (p >> (k + 1)) == (pp >> (k + 1))
        sets.append(steps & same & (((p >> k) & 1) == 1) & (((pp >> k) & 1) == 0))
    sets.append((j == 3) & (jj < 3))
    for k, chosen in enumerate(sets):
        masks[k] = chosen.astype(F32)
    strict = steps & ((p > pp) | ((p == pp) & (j > jj)))
    masks[LEVELS + 1] = (strict | ((j == 3) & (jj < 3) & (p >= pp))).astype(F32)
    tri[...] = ((j == jj) & (pp <= p)).astype(F32)
    for c in range(NC):
        picks[:, c * N : (c + 1) * N] = ((j == c) & (p <= pp)).astype(F32)


def silu(v):
    return v / (1.0 + jnp.exp(-v))


def softplus(v):
    return jnp.maximum(v, 0.0) + jnp.log1p(jnp.exp(-jnp.abs(v)))


def place_rates(rate_t, weight, blank):
    width = weight.shape[1] - N
    blank[...] = jnp.zeros((N, N), F32)
    for b in range(rate_t.shape[1] // N):
        blank[0:4, :] = rate_t[:, b * N : (b + 1) * N].astype(F32)
        weight[b * N : (b + 1) * N, width:] = blank[...].T.astype(BF)


def widen(owners, fresh, blocks, gain, xs, squares):
    total = None
    for k, owner in enumerate(owners):
        for core in range(2):
            wide = blocks[owner * 2 + core].astype(F32)
            total = wide * wide if total is None else total + wide * wide
            at = (2 * k + core) * N
            xs[:, at : at + N] = (wide * gain[pl.ds(owner * 2 + core, 1), :]).astype(BF)
    squares[...] = total if fresh else squares[...] + total


def absorb(owners, fresh, half, weight, xs, acc):
    cols = slice(half * 4 * N, (half + 1) * 4 * N)
    kernel = jnp.concatenate(
        [weight[pl.ds(pl.multiple_of(o * 2 * N, 2 * N), 2 * N), cols] for o in owners], axis=0
    )
    product = dot(xs[:, : 2 * N * len(owners)], kernel)
    acc[:, cols] = product if fresh else acc[:, cols] + product


def sequence_inputs(s, length, rate, count, acc, squares, masks, tri, picks, la, tt, tmp, xh, xl, kt, eq, et):
    rows = slice(s * N, (s + 1) * N)
    total = jnp.sum(squares[rows, :], axis=1, keepdims=True)
    inverse = lax.rsqrt(total / (count * N) + ROW_EPSILON)
    projected = acc[rows, : 7 * N] * inverse
    rates = acc[rows, 7 * N :] * inverse
    query = silu(projected[:, :N])
    keys, values = [], []
    for j in range(3):
        key = silu(projected[:, (1 + j) * N : (2 + j) * N])
        keys.append(key * lax.rsqrt(jnp.sum(key * key, axis=1, keepdims=True) + KEY_EPSILON))
        values.append(silu(projected[:, (4 + j) * N : (5 + j) * N]))
    valid = lax.broadcasted_iota(jnp.int32, (N, 1), 0) < length
    betas = [
        jnp.broadcast_to(jnp.where(valid, 2.0 * jax.nn.sigmoid(rates[:, j : j + 1]), 0.0), (N, N))
        for j in range(3)
    ]
    decay = jnp.where(valid, -rate * softplus(rates[:, 3:4]), 0.0)
    decay = jnp.broadcast_to(decay, (N, N))
    cum = jnp.dot(tri[...], decay, precision=HI, preferred_element_type=F32)
    cum_row = jnp.dot(decay.T[:8], picks[...], precision=HI, preferred_element_type=F32)
    grow = jnp.exp(cum)
    one = jnp.ones((CH, N), F32)
    zero = jnp.zeros((CH, N), F32)
    eye = (
        lax.broadcasted_iota(jnp.int32, (N, N), 0) == lax.broadcasted_iota(jnp.int32, (N, N), 1)
    ).astype(F32)
    causal = masks[LEVELS + 1] > 0.5
    first = masks[0]
    for c in range(NC):
        at = slice(c * CH, (c + 1) * CH)
        n = s * NC + c
        kq = jnp.concatenate([keys[0][at], keys[1][at], keys[2][at], query[at]], axis=0)
        vv = jnp.concatenate([values[0][at], values[1][at], values[2][at], zero], axis=0)
        bb = jnp.concatenate([betas[0][at], betas[1][at], betas[2][at], one], axis=0)
        cc = jnp.concatenate([cum[at]] * 4, axis=0)
        gg = jnp.concatenate([grow[at]] * 3 + [zero], axis=0)
        high, low = split(kq)
        gram = halves(
            dot_nt(
                jnp.concatenate([high, low], axis=1),
                jnp.concatenate(
                    [jnp.concatenate([high, high], axis=1), jnp.concatenate([low, low], axis=1)],
                    axis=0,
                ),
            )
        )
        ratio = jnp.exp(jnp.where(causal, cc - cum_row[0:1, c * N : (c + 1) * N], -1e30))
        system = bb * ratio * gram
        la[n] = system
        pairs = system * first
        scale = jnp.sum(pairs[CH : 2 * CH], axis=0, keepdims=True)
        third = system[2 * CH : 3 * CH] * masks[1, 2 * CH : 3 * CH, :]
        third = third - pltpu.roll(third, N - CH, 1) * scale
        start = eye - pairs
        tt[n] = jnp.concatenate([start[: 2 * CH], start[2 * CH : 3 * CH] - third, start[3 * CH :]], axis=0)
        tmp[n] = jnp.zeros((N, N), F32)
        xa, xb = bb * vv, bb * gg * kq
        ha, lo_a = split(xa)
        hb, lo_b = split(xb)
        xh[n] = jnp.concatenate([ha, hb], axis=1)
        xl[n] = jnp.concatenate([lo_a, lo_b], axis=1)
        last = cum[(c + 1) * CH - 1 : (c + 1) * CH, :]
        tail = jnp.concatenate([jnp.exp(last - cum[at])] * 3 + [zero], axis=0)
        kt[n] = left_of((tail * kq).T)
        eq[n] = grow[at] * query[at]
        et[n] = jnp.broadcast_to(jnp.exp(last), (8, N))


def invert(ids, first, stop, masks, la, tt, tmp):
    top = 3 * CH

    def level(k, carry):
        mask = masks[k, :top, :]
        for n in ids:
            tmp[n, :top, :] = halves(dot(left_of(la[n, :top, :] * mask), right_of(tt[n])))
        for n in ids:
            t = tt[n, :top, :]
            tt[n, :top, :] = t - halves(dot(left_of(t), right_of(tmp[n])))
        return carry

    lax.fori_loop(first, stop, level, 0)
    if stop < LEVELS:
        return
    for n in ids:
        tt[n, top:, :] = -halves(dot(left_of(la[n, top:, :]), right_of(tt[n])))


def chunk_maps(n, tt, xh, xl, kt, eq, et, pq, rr, ov):
    high, low = split(tt[n])
    big = jnp.concatenate([high, low], axis=1)
    z = dot(big, jnp.concatenate([xh[n], xh[n]], axis=0)) + dot(high, xl[n])
    zh, zl = split(z)
    k = kt[n]
    maps = dot(k, jnp.concatenate([zh, zh], axis=0)) + dot(k[:, :N], zl)
    eye = (
        lax.broadcasted_iota(jnp.int32, (N, N), 0) == lax.broadcasted_iota(jnp.int32, (N, N), 1)
    ).astype(F32)
    p = eye * et[n, 0:1, :] - maps[:, N:]
    pq[n] = left_of(jnp.concatenate([p, eq[n] + z[3 * CH :, N:]], axis=0))
    rr[n] = maps[:, :N]
    ov[n] = -z[3 * CH :, :N]


def run_chain(sequences, states, new_state, normed, head_gain, pq, rr, ov):
    carried = [states[s].T for s in sequences]
    for c in range(NC):
        for k, s in enumerate(sequences):
            n = s * NC + c
            both = halves(dot(pq[n], right_of(carried[k])))
            carried[k] = both[:N] + rr[n]
            attended = both[N:] + ov[n]
            factor = lax.rsqrt(jnp.mean(attended * attended, axis=1, keepdims=True) + ROW_EPSILON)
            normed[s * N + c * CH : s * N + (c + 1) * CH, :] = (
                attended * factor * head_gain[...]
            ).astype(BF)
    for k, s in enumerate(sequences):
        new_state[s] = carried[k].T


def mixer_scratch(seqs, count, width):
    m = seqs * NC
    return [
        pltpu.VMEM((LEVELS + 2, N, N), F32),
        pltpu.VMEM((N, N), F32),
        pltpu.VMEM((N, NC * N), F32),
        pltpu.VMEM((seqs * N, 4 * N), BF),
        pltpu.VMEM((seqs * N, 8 * N), F32),
        pltpu.VMEM((seqs * N, N), F32),
        pltpu.VMEM((m, N, N), F32),
        pltpu.VMEM((m, N, N), F32),
        pltpu.VMEM((m, N, N), F32),
        pltpu.VMEM((m, N, 2 * N), BF),
        pltpu.VMEM((m, N, 2 * N), BF),
        pltpu.VMEM((m, N, 2 * N), BF),
        pltpu.VMEM((m, CH, N), F32),
        pltpu.VMEM((m, 8, N), F32),
        pltpu.VMEM((m, N + CH, 2 * N), BF),
        pltpu.VMEM((m, N, N), F32),
        pltpu.VMEM((m, CH, N), F32),
    ]


SEQS = 4
PARTS = 4
VOCAB_HERE = 32
SOURCES = 32
Z, X, Y, C = "batch_0", "batch_1", "head_0", "head_1"
HEAD = (Y, C)
BATCH = (Z, X)
BATCH_HEAD = (Z, X, Y, C)
MESH = pl.DeviceIdType.MESH


def remote(src, dst, send_sem, recv_sem, **place):
    return pltpu.make_async_remote_copy(
        src_ref=src,
        dst_ref=dst,
        send_sem=send_sem,
        recv_sem=recv_sem,
        device_id=place,
        device_id_type=MESH,
    )


def send(src, dst, send_sem, recv_sem, **place):
    copy = remote(src, dst, send_sem, recv_sem, **place)
    copy.start()
    return copy


def arrived(dst, recv_sem):
    pltpu.make_async_remote_copy(
        src_ref=dst,
        dst_ref=dst,
        send_sem=recv_sem,
        recv_sem=recv_sem,
        device_id={C: lax.axis_index(C)},
        device_id_type=MESH,
    ).wait_recv()


def wrap(index, size):
    return lax.rem(index + size, size)


class Ring:
    def __init__(self, buf, sems, ny):
        self.buf, self.ny = buf, ny
        self.s_right, self.r_right, self.s_left, self.r_left, self.s_pair, self.r_pair = sems
        self.y, self.c = lax.axis_index(Y), lax.axis_index(C)
        long, short = ny // 2, (ny - 1) // 2
        self.steps = [(long, short) if s % 2 == 0 else (short, long) for s in range(PARTS)]
        self.last = long - 1

    def piece(self, owner, core, s):
        size = self.buf.shape[1] // PARTS
        return self.buf.at[owner * 2 + core, pl.ds(s * size, size), :]

    def owner(self, way, k):
        return wrap(self.y - (k + 1), self.ny) if way == 0 else wrap(self.y + (k + 1), self.ny)

    def pair_index(self, way, k, s):
        return (1 + k if way == 0 else 1 + self.steps[s][0] + k) * PARTS + s

    def hop(self, way, k, s):
        piece = self.piece(self.owner(way, k - 1), self.c, s)
        to = wrap(self.y + 1, self.ny) if way == 0 else wrap(self.y - 1, self.ny)
        ss, rs = (self.s_right, self.r_right) if way == 0 else (self.s_left, self.r_left)
        at = k * PARTS + s
        return remote(piece, piece, ss.at[at], rs.at[at], **{Y: to})

    def to_pair(self, way, k, s):
        piece = self.piece(self.owner(way, k), self.c, s)
        at = self.pair_index(way, k, s)
        return remote(piece, piece, self.s_pair.at[at], self.r_pair.at[at], **{C: 1 - self.c})

    def start(self):
        for s in range(PARTS):
            for way in range(2):
                if self.steps[s][way] > 0:
                    self.hop(way, 0, s).start()
        for s in range(PARTS):
            self.to_pair(0, -1, s).start()

    def forward(self, k, s):
        for way in range(2):
            if k < self.steps[s][way]:
                owner = self.owner(way, k)
                at = k * PARTS + s
                arrived(self.piece(owner, self.c, s), (self.r_right, self.r_left)[way].at[at])
                if k + 1 < self.steps[s][way]:
                    self.hop(way, k + 1, s).start()
                self.to_pair(way, k, s).start()

    def step(self, k):
        for s in range(PARTS):
            self.forward(k, s)

    def wait_pair(self, way, k):
        for s in range(PARTS):
            at = way if k < self.steps[s][way] else 1 - way
            piece = self.piece(self.owner(at, k), 1 - self.c, s)
            arrived(piece, self.r_pair.at[self.pair_index(at, k, s)])

    def owners(self, k):
        return [(0, k), (1, k)] if 2 * (k + 1) < self.ny else [(0, k)]

    def wait_all_pairs(self):
        self.wait_pair(0, -1)
        for k in range(self.last + 1):
            for way, step in self.owners(k):
                self.wait_pair(way, step)

    def drain(self):
        for s in range(PARTS):
            self.to_pair(0, -1, s).wait_send()
            for way in range(2):
                for k in range(self.steps[s][way]):
                    self.hop(way, k, s).wait_send()
                    self.to_pair(way, k, s).wait_send()


def exchange_head(buf, mine, sems, ny):
    y, c = lax.axis_index(Y), lax.axis_index(C)
    sent = []
    order = sorted(range(1, 2 * ny), key=lambda k: -min(k // 2, ny - k // 2))
    for k in order:
        to = {Y: wrap(y + k // 2, ny), C: lax.rem(c + k % 2, 2)}
        sent.append(send(buf.at[mine], buf.at[mine], sems[0].at[k - 1], sems[1].at[k - 1], **to))
    return sent


def await_head(buf, sems, ny):
    y, c = lax.axis_index(Y), lax.axis_index(C)
    for k in range(1, 2 * ny):
        source = wrap(y - k // 2, ny) * 2 + lax.rem(c + k % 2, 2)
        arrived(buf.at[source], sems[1].at[k - 1])


def exchange_axis(axis, size, piece, sems):
    me = lax.axis_index(axis)
    order = sorted(range(1, size), key=lambda k: -min(k, size - k))
    return [
        send(piece(me), piece(me), sems[0].at[k - 1], sems[1].at[k - 1], **{axis: wrap(me + k, size)})
        for k in order
    ]


def await_axis(axis, size, piece, sems):
    me = lax.axis_index(axis)
    for k in range(1, size):
        arrived(piece(wrap(me - k, size)), sems[1].at[k - 1])


def combine(buf, count):
    parts = [buf[k] for k in range(count)]
    top = functools.reduce(jnp.maximum, [part[0:1] for part in parts])
    total = sum(part[1:2] * jnp.exp(part[0:1] - top) for part in parts)
    target = sum(part[2:3] for part in parts)
    return top, total, target


def put_stats(buf, at, top, total, target):
    buf[at] = jnp.concatenate([top, total, target, jnp.zeros_like(top)], axis=0)


NAMES = (
    "masks", "tri", "picks", "xs", "acc", "squares", "la", "tt", "tmp", "xh", "xl", "kt", "eq", "et", "pq",
    "rr", "ov", "blocks", "nall", "weight", "cols", "vocab", "state", "blank", "lastn",
    "lastm", "shaped", "hid", "part", "other", "sy", "sp", "tr1", "tr2", "tr3", "tr4",
    "tr5", "tr6", "nr1", "nr2", "nr3", "nr4", "nr5", "nr6", "c1", "c2", "d1", "d2", "v1", "v2", "a1",
    "a2", "b1", "b2", "z1", "z2", "x1", "x2", "p1", "p2", "g1", "g2", "h1", "h2",
    "local", "free", "gain", "rates", "hgain", "fgain", "wanted", "length", "rate",
)


def one_kernel(sizes, *refs):
    (tokens, lengths_in, states, gain_in, mix_weight, rate_in, decay_in, head_in, out_weight,
     final_in, vocab_table, next_in, mixed, new_state, likelihood) = refs[:15]
    r = dict(zip(NAMES, refs[15:]))
    nz, nx, ny = sizes
    heads = 2 * ny
    z, x, y, c = (lax.axis_index(a) for a in BATCH_HEAD)
    me = y * 2 + c
    blocks, nall, cols, hid = r["blocks"], r["nall"], r["cols"], r["hid"]
    local = r["local"]
    gain, rate_t, head_gain, final_gain = r["gain"], r["rates"], r["hgain"], r["fgain"]
    next_token, lengths, rate = r["wanted"], r["length"], r["rate"]
    weight, acc, squares_of = r["weight"], r["acc"], r["squares"]

    own = pltpu.make_async_copy(tokens, blocks.at[me], local.at[0])
    own.start()
    small = []
    for k, (src, dst) in enumerate((
        (gain_in, gain), (rate_in, rate_t), (head_in, head_gain), (final_in, final_gain),
        (next_in, next_token), (lengths_in, lengths), (decay_in, rate),
    )):
        small.append(pltpu.make_async_copy(src, dst, local.at[8 + k]))
        small[-1].start()
    load_weight = pltpu.make_async_copy(mix_weight, weight.at[:, pl.ds(0, 7 * N)], local.at[1])
    load_weight.start()
    load_state = pltpu.make_async_copy(states, r["state"], local.at[2])
    load_state.start()
    band = N // nx
    rows_here = pl.ds(pl.multiple_of(x * band, band), band)
    own_cols = pltpu.make_async_copy(
        out_weight.at[rows_here, pl.ds(pl.multiple_of(me * N, N), N)],
        cols.at[me, rows_here, :],
        local.at[3],
    )
    own_cols.start()
    quarter = heads * N // 8
    vocab_copies = []

    def vocab_piece(half, q):
        start = pl.multiple_of(half * (4 * quarter) + q * quarter, N)
        rows = pl.ds(pl.multiple_of(q * 2 * VOCAB_HERE + c * VOCAB_HERE, VOCAB_HERE), VOCAB_HERE)
        return vocab_table.at[:, pl.ds(start, quarter)], r["vocab"].at[rows, :]

    for q in range(4):
        src, dst = vocab_piece(c, q)
        copy = pltpu.make_async_copy(src, dst, local.at[4 + q])
        copy.start()
        vocab_copies.append(copy)
    if nz * nx < SOURCES:
        hid[...] = jnp.zeros_like(hid)

    barrier = pltpu.get_barrier_semaphore()
    near = [{C: 1 - c}]
    for axis, size, at in ((Y, ny, y), (Z, nz, z), (X, nx, x)):
        if size > 1:
            near += [{axis: wrap(at + 1, size)}, {axis: wrap(at - 1, size)}]
    for place in near:
        pl.semaphore_signal(barrier, inc=1, device_id=place, device_id_type=MESH)
    own.wait()
    pl.semaphore_wait(barrier, len(near))

    ring = Ring(blocks, [r[f"tr{k}"] for k in range(1, 7)], ny)
    ring.start()
    pair_vocab = []
    for q in range(4):
        src, dst = vocab_piece(1 - c, q)
        pair_vocab.append(send(src, dst, r["v1"].at[q], r["v2"].at[q], **{C: 1 - c}))

    pending = []
    free = r["free"]
    for slot, (axis, size, at) in enumerate(((X, nx, x), (Z, nz, z))):
        for _ in range(size - 1):
            def signal(slot=slot, axis=axis, size=size, at=at):
                pl.semaphore_signal(
                    free.at[slot], inc=1, device_id={axis: wrap(at + 1, size)}, device_id_type=MESH
                )

            def await_signal(slot=slot):
                pl.semaphore_wait(free.at[slot], 1)

            pending += [signal, await_signal]

    def plane_step():
        if pending:
            pending.pop(0)()

    def plane_next():
        plane_step()
        plane_step()

    if pending:
        plane_step()
    fill_tables(r["masks"], r["tri"], r["picks"])
    for copy in small:
        copy.wait()
    place_rates(rate_t, weight, r["blank"])
    load_weight.wait()

    def ready(arrivals):
        for way, k in arrivals:
            ring.wait_pair(way, k)
        owners = [ring.owner(way, k) for way, k in arrivals]
        fresh = arrivals[0][1] < 0
        widen(owners, fresh, blocks, gain, r["xs"], squares_of)
        return owners, fresh

    def take(owners, fresh, half):
        absorb(owners, fresh, half, weight, r["xs"], acc)

    for k in range(ring.last + 1):
        half = PARTS // 2
        for s in range(half):
            ring.forward(k, s)
        found = ready([(0, -1)] if k == 0 else ring.owners(k - 1))
        take(*found, 0)
        for s in range(half, PARTS):
            ring.forward(k, s)
        take(*found, 1)
        plane_next()

    col_sent = []
    for k in range(1, heads):
        py, pc = wrap(y + k // 2, ny), lax.rem(c + k % 2, 2)
        to = pl.multiple_of((py * 2 + pc) * N, N)
        col_sent.append(
            send(out_weight.at[rows_here, pl.ds(to, N)], cols.at[me, rows_here, :],
                 r["c1"].at[k - 1], r["c2"].at[k - 1], **{Y: py, C: pc})
        )
    found = ready(ring.owners(ring.last))
    take(*found, 0)
    take(*found, 1)
    for s in range(SEQS):
        plane_next()
        sequence_inputs(
            s, lengths[s], rate[0], heads, acc, squares_of, r["masks"], r["tri"], r["picks"],
            r["la"], r["tt"], r["tmp"], r["xh"], r["xl"], r["kt"], r["eq"], r["et"],
        )
    plane_next()
    ids = range(SEQS * NC)
    invert(ids, 2, 5, r["masks"], r["la"], r["tt"], r["tmp"])
    plane_next()
    own_cols.wait()
    for k in range(1, heads):
        source = wrap(y - k // 2, ny) * 2 + lax.rem(c + k % 2, 2)
        arrived(cols.at[source, rows_here, :], r["c2"].at[k - 1])
    bands = cols.at[:, rows_here, :]
    for dx in range(1, nx):
        col_sent.append(
            send(bands, bands, r["d1"].at[dx - 1], r["d2"].at[dx - 1], **{X: wrap(x + dx, nx)})
        )
    invert(ids, 5, LEVELS, r["masks"], r["la"], r["tt"], r["tmp"])
    plane_next()
    for n in ids:
        chunk_maps(
            n, r["tt"], r["xh"], r["xl"], r["kt"], r["eq"], r["et"], r["pq"], r["rr"], r["ov"]
        )
    load_state.wait()
    plane_next()
    run_chain(
        range(SEQS), r["state"], new_state, nall.at[me], head_gain, r["pq"], r["rr"], r["ov"]
    )

    position = lax.broadcasted_iota(jnp.int32, (N, N), 0)

    def last_rows(ref):
        rows = []
        for s in range(SEQS):
            wide = ref[me, s * N : (s + 1) * N, :].astype(F32)
            kept = jnp.where(position == lengths[s] - 1, wide, 0.0)
            rows.append(jnp.sum(kept, axis=0, keepdims=True))
        return jnp.concatenate(rows, axis=0)

    lastn, lastm = r["lastn"], r["lastm"]
    lastn[me] = last_rows(nall)
    sends = exchange_head(lastn, me, (r["a1"], r["a2"]), ny)
    bulk = Ring(nall, [r[f"nr{k}"] for k in range(1, 7)], ny)
    residual = last_rows(blocks)
    for dx in range(1, nx):
        theirs = pl.ds(pl.multiple_of(wrap(x - dx, nx) * band, band), band)
        arrived(cols.at[:, theirs, :], r["d2"].at[dx - 1])
    await_head(lastn, (r["a1"], r["a2"]), ny)
    wide = jnp.concatenate([lastn[b].astype(BF) for b in range(heads)], axis=1)
    every_col = jnp.concatenate([cols[b] for b in range(heads)], axis=0)
    lastm[me] = (residual + dot(wide, every_col)).astype(BF).astype(F32)
    sends += exchange_head(lastm, me, (r["b1"], r["b2"]), ny)
    bulk.start()
    late = list(range(ring.last + 1))

    def bulk_step():
        if late:
            bulk.step(late.pop(0))

    while pending:
        plane_step()
    await_head(lastm, (r["b1"], r["b2"]), ny)
    squares = sum(lastm[b] * lastm[b] for b in range(heads))
    factor = lax.rsqrt(jnp.sum(squares, axis=1, keepdims=True) / (heads * N) + ROW_EPSILON)
    per = heads // 8
    shaped = r["shaped"]
    for q in range(4):
        for k in range(per):
            b = c * (heads // 2) + q * per + k
            shaped[q * SEQS : (q + 1) * SEQS, k * N : (k + 1) * N] = (
                lastm[b] * factor * final_gain[pl.ds(b, 1), :]
            )
    slot = x * nz + z
    hid[slot] = shaped[...].astype(BF)
    def cell(px, pz):
        return hid.at[px * nz + pz]

    def to_row(pz, k):
        for dx in range(1, nx):
            at = (dx - 1) * nz + k
            sends.append(
                send(cell(x, pz), cell(x, pz), r["x1"].at[at], r["x2"].at[at], **{X: wrap(x + dx, nx)})
            )

    sends += exchange_axis(Z, nz, lambda pz: cell(x, pz), (r["z1"], r["z2"]))
    to_row(z, 0)
    bulk_step()
    for k in sorted(range(1, nz), key=lambda k: min(k, nz - k)):
        pz = wrap(z - k, nz)
        arrived(cell(x, pz), r["z2"].at[k - 1])
        to_row(pz, k)
    bulk_step()
    for q in range(4):
        vocab_copies[q].wait()
        rows = pl.ds(
            pl.multiple_of(q * 2 * VOCAB_HERE + (1 - c) * VOCAB_HERE, VOCAB_HERE), VOCAB_HERE
        )
        arrived(r["vocab"].at[rows, :], r["v2"].at[q])
    lane = lax.broadcasted_iota(jnp.int32, (N, N), 1)
    rank = lax.broadcasted_iota(jnp.int32, (N, N), 0)
    source = ((lane // 4) % 4) * 8 + lane // 16
    order = (lax.rem(source, nz) * nx + source // nz) * SEQS + lane % 4
    permute = ((order == rank) & (source < nz * nx)).astype(F32)
    wanted = jnp.broadcast_to(next_token[...].astype(F32), (8, N))
    wanted = jnp.dot(wanted, permute, precision=HI, preferred_element_type=F32)[0:1]
    wanted = (wanted + 0.5).astype(jnp.int32)
    for dx in range(1, nx):
        for k in range(nz):
            arrived(cell(wrap(x - dx, nx), wrap(z - k, nz)), r["x2"].at[(dx - 1) * nz + k])

    everyone = jnp.concatenate([hid[k] for k in range(SOURCES)], axis=0)
    product = dot_nt(r["vocab"][...], everyone)
    height = 2 * VOCAB_HERE
    quarter_of = (lane[:height] % 16) // 4
    packed = jnp.zeros((height, N), F32)
    for k in range(4):
        mine = jnp.zeros((height, N), F32)
        for q in range(4):
            block = product[q * height : (q + 1) * height, k * N : (k + 1) * N]
            mine = mine + jnp.where(quarter_of == q, block, 0.0)
        mine = mine + pltpu.roll(mine, N - 4, 1)
        mine = mine + pltpu.roll(mine, N - 8, 1)
        if k:
            mine = pltpu.roll(mine, 4 * k, 1)
        packed = packed + jnp.where(quarter_of == k, mine, 0.0)
    part, other = r["part"], r["other"]
    part[0] = packed[:VOCAB_HERE]
    part[1] = packed[VOCAB_HERE:]
    sends.append(send(part.at[1 - c], other, r["p1"].at[0], r["p2"].at[0], **{C: 1 - c}))
    arrived(other, r["p2"].at[0])
    logits = part[c] + other[...]
    vocab_ids = (((z * nx + x) * ny + y) * 2 + c) * VOCAB_HERE + rank[:VOCAB_HERE]
    top = jnp.max(logits, axis=0, keepdims=True)
    total = jnp.sum(jnp.exp(logits - top), axis=0, keepdims=True)
    target = jnp.sum(jnp.where(vocab_ids == wanted, logits, 0.0), axis=0, keepdims=True)
    sy, sp = r["sy"], r["sp"]
    put_stats(sy, me, top, total, target)
    sends += exchange_head(sy, me, (r["g1"], r["g2"]), ny)
    bulk_step()
    await_head(sy, (r["g1"], r["g2"]), ny)
    put_stats(sp, slot, *combine(sy, heads))
    far = sorted(
        (k for k in range(1, nz * nx)),
        key=lambda k: -min(k % nz, nz - k % nz) - min(k // nz, nx - k // nz),
    )
    for k in far:
        to = {Z: wrap(z + k % nz, nz), X: wrap(x + k // nz, nx)}
        sends.append(send(sp.at[slot], sp.at[slot], r["h1"].at[k - 1], r["h2"].at[k - 1], **to))
    while late:
        bulk_step()
    bulk.wait_all_pairs()

    def mix(s, carry):
        rows = pl.ds(pl.multiple_of(s * N, N), N)
        wide = jnp.concatenate([nall[b, rows, :] for b in range(heads)], axis=1)
        every = jnp.concatenate([cols[b] for b in range(heads)], axis=0)
        mixed[rows, :] = (blocks[me, rows, :].astype(F32) + dot(wide, every)).astype(BF)
        return carry

    lax.fori_loop(0, SEQS, mix, 0)
    ring.drain()
    bulk.drain()
    for copy in col_sent + pair_vocab:
        copy.wait_send()
    for k in range(1, nz * nx):
        arrived(sp.at[wrap(x - k // nz, nx) * nz + wrap(z - k % nz, nz)], r["h2"].at[k - 1])
    top, total, target = combine(sp, nz * nx)
    result = jnp.broadcast_to(target - (top + jnp.log(total)), (8, N))
    likelihood[...] = lax.dot_general(
        result, permute, (((1,), (1,)), ((), ())), precision=HI, preferred_element_type=F32
    )[0:1]
    for copy in sends:
        copy.wait_send()


def deliver_kernel(*refs):
    sems = refs[-1]
    copies = [pltpu.make_async_copy(refs[k], refs[3 + k], sems.at[k]) for k in range(3)]
    for copy in copies:
        copy.start()
    for copy in copies:
        copy.wait()


def deliver(*arrays):
    return pl.pallas_call(
        deliver_kernel,
        out_shape=tuple(jax.ShapeDtypeStruct(a.shape, a.dtype) for a in arrays),
        in_specs=[pl.BlockSpec(memory_space=pltpu.VMEM)] * 3,
        out_specs=(pl.BlockSpec(memory_space=pl.ANY),) * 3,
        scratch_shapes=[pltpu.SemaphoreType.DMA((3,))],
    )(*arrays)


def on_device(sizes, tokens, lengths, states, norm_gain, mix_weight, rate_weight, decay_rate,
              head_gain, out_weight, final_gain, vocab_table, next_token):
    nz, nx, ny = sizes
    heads = 2 * ny
    rows = SEQS * N
    everyone = next_token.shape[0]
    vmem = pl.BlockSpec(memory_space=pltpu.VMEM)
    hbm = pl.BlockSpec(memory_space=pltpu.HBM)
    dma = lambda n: pltpu.SemaphoreType.DMA((max(n, 1),))
    group = 2 * ny - 1
    scratch = mixer_scratch(SEQS, heads, mix_weight.shape[1]) + [
        pltpu.VMEM((heads, rows, N), BF),
        pltpu.VMEM((heads, rows, N), BF),
        pltpu.VMEM((heads * N, 8 * N), BF),
        pltpu.VMEM((heads, N, N), BF),
        pltpu.VMEM((8 * VOCAB_HERE, heads * N // 8), BF),
        pltpu.VMEM((SEQS, N, N), F32),
        pltpu.VMEM((N, N), F32),
        pltpu.VMEM((heads, SEQS, N), F32),
        pltpu.VMEM((heads, SEQS, N), F32),
        pltpu.VMEM((4 * SEQS, heads * N // 8), F32),
        pltpu.VMEM((SOURCES, 4 * SEQS, heads * N // 8), BF),
        pltpu.VMEM((2, VOCAB_HERE, N), F32),
        pltpu.VMEM((VOCAB_HERE, N), F32),
        pltpu.VMEM((heads, 4, N), F32),
        pltpu.VMEM((nz * nx, 4, N), F32),
    ]
    hops = PARTS * max(ny // 2, 1)
    scratch += [dma(hops)] * 4 + [dma(PARTS * ny)] * 2
    scratch += [dma(hops)] * 4 + [dma(PARTS * ny)] * 2
    scratch += [dma(group)] * 2 + [dma(nx - 1)] * 2 + [dma(4)] * 2 + [dma(group)] * 4
    scratch += [dma(nz - 1)] * 2 + [dma((nx - 1) * nz)] * 2 + [dma(1)] * 2
    scratch += [dma(group)] * 2 + [dma(nz * nx - 1)] * 2
    scratch += [dma(15), pltpu.SemaphoreType.REGULAR((2,))]
    scratch += [
        pltpu.VMEM((heads, N), F32),
        pltpu.VMEM((4, heads * N), BF),
        pltpu.VMEM((1, N), F32),
        pltpu.VMEM((heads, N), F32),
        pltpu.VMEM((1, N), jnp.int32),
        pltpu.SMEM((SEQS,), jnp.int32),
        pltpu.SMEM((1,), F32),
    ]
    wanted = next_token.reshape(1, everyone)
    if everyone < N:
        wanted = jnp.pad(wanted, ((0, 0), (0, N - everyone)))
    mixed, new_state, likelihood = pl.pallas_call(
        functools.partial(one_kernel, sizes),
        out_shape=(
            jax.ShapeDtypeStruct((rows, N), BF),
            jax.ShapeDtypeStruct((SEQS, N, N), F32),
            jax.ShapeDtypeStruct((1, N), F32),
        ),
        in_specs=[hbm] * 12,
        out_specs=(vmem, vmem, vmem),
        scratch_shapes=scratch,
        compiler_params=pltpu.CompilerParams(
            collective_id=0, has_side_effects=True, vmem_limit_bytes=63 * 1024 * 1024
        ),
    )(
        tokens,
        lengths,
        states[:, 0],
        norm_gain.reshape(heads, N),
        mix_weight,
        rate_weight.T,
        decay_rate,
        head_gain.reshape(1, N),
        out_weight,
        final_gain.reshape(heads, N),
        vocab_table,
        wanted,
    )
    mixed, new_state, likelihood = deliver(mixed, new_state, likelihood)
    return mixed, new_state[:, None], likelihood[0, :everyone]


def build(torus):
    sizes = (torus.shape[Z], torus.shape[X], torus.shape[Y])
    placed = (
        P(BATCH, HEAD),
        P(BATCH),
        P(BATCH, HEAD, None, None),
        P(),
        P(None, HEAD),
        P(None, HEAD),
        P(HEAD),
        P(),
        P(HEAD, None),
        P(),
        P(BATCH_HEAD, None),
        P(),
    )
    return jax.shard_map(
        functools.partial(on_device, sizes),
        mesh=torus,
        in_specs=placed,
        out_specs=(P(BATCH, HEAD), P(BATCH, HEAD, None, None), P()),
        check_vma=False,
    )


def solution(mesh):
    torus = Mesh(mesh.devices.reshape(8, 4, 8, 2), BATCH_HEAD)
    return build(torus)
```

time: 262 us -> 80.3 us (0.31)
  blocking collectives: 126 us -> 0 us
  waiting for transfers between devices: 90.3 us -> 0 us
  Pallas kernels: 19.6 us -> 78.7 us
  between operations: 14.9 us -> 1.45 us
  starting transfers between devices: 4.94 us -> 0 us
  matrix products: 2.77 us -> 0 us
    all_gather x5 -> x0, blocking collectives: 126 us -> none  [the longest x1 70.3 us: on_device(): gathered = lax.all_gather(last_rows[None], BATCH_HEAD, axis=0, tiled=True)]
    all_gather x2 -> x0, waiting for transfers between devices: 71 us -> none  [the longest x1 49.2 us: on_device(): blocks = lax.all_gather(tokens, HEAD, axis=0)]
    pallas_call x1 -> x2, Pallas kernels: 19.6 us -> 78.7 us  [the longest x1 77 us: on_device(): pl.pallas_call(functools.partial(one_kernel, sizes), out_shape=(jax.Shape...]
    all_to_all x1 -> x0, waiting for transfers between devices: 18.5 us -> none  [on_device(): lax.all_to_all(out_weight, HEAD, split_axis=1, concat_axis=0, tiled=True)]
    all_to_all x1 -> x0, starting transfers between devices: 4.87 us -> none  [on_device(): lax.all_to_all(out_weight, HEAD, split_axis=1, concat_axis=0, tiled=True)]
    dot_general x2 -> x0, matrix products: 2.77 us -> none  [the longest x1 2.3 us: on_device(): jnp.dot(lax.all_gather(normed, HEAD, axis=1, tiled=True), columns, prefer...]
  transfers between devices with their start and end apart: 3 -> 0, of which waited for: 3 -> 0; matrix products, arithmetic and copies ran while one was open for 1% -> 0% of each run, Pallas kernels for 0% -> 0%
where the time goes in v2:
time: 80.3 us; the launch traced here: 80.2 us
  Pallas kernels  78.7 us (98%)
  between operations  1.45 us (2%)
    pallas_call x1, Pallas kernels, on_device(): pl.pallas_call(functools.partial(one_kernel, sizes), out_shape=(jax.Shape...  77 us
    pallas_call x1, Pallas kernels, deliver(): pl.pallas_call(deliver_kernel, out_shape=tuple((jax.ShapeDtypeStruct(a.sh...  1.76 us

profile of v2, /device:TPU:1, one launch (start us, length us, event | category | flops | bytes accessed | tf_op | source)
XLA Modules:
  0.0 80.2 jit_solution(14573135485509651013)
XLA Ops:
  1.3 77.0 %shard_map.139 = (bf16[512,128]{1,0:T(8,128)(2,1)}, f32[4,128,128]{2,1,0:T(8,128)}, f32[1,128]{1,0:T(1,128)}) custom-call(bf16[512,128]{1,0:T(8,128)(2,1)} %refs_0_.1, s32[4]{0:T(128)} %refs_1_.1, f32[4,128,128]{2,1,0:T(8,128)} %bitcast.10, f32[16,128]{1,0:T(8,128)} %bitcast.12, bf16[2048,896]{1,0:T(8,128)(2,1)} %refs_4_.1, bf16[4,2048]{1,0:T(4,128)(2,1)} %bitcast.11, ...), custom_call_target="tpu_custom_call" | custom-call | tf_op jit(solution)/shard_map/pallas_call | solution.py:794
  78.3 1.8 %shard_map.140 = (bf16[512,128]{1,0:T(8,128)(2,1)}, f32[4,128,128]{2,1,0:T(8,128)}, f32[1,128]{1,0:T(1,128)}) custom-call(bf16[512,128]{1,0:T(8,128)(2,1)} %get-tuple-element.9.refs_0_, f32[4,128,128]{2,1,0:T(8,128)} %get-tuple-element.10.refs_1_, f32[1,128]{1,0:T(1,128)} %get-tuple-element.11.refs_2_), custom_call_target="tpu_custom_call" | custom-call | tf_op jit(solution)/shard_map/pallas_call | solution.py:739

commit v3 on v2

--- a/solution.py
+++ b/solution.py
@@ -28,10 +28,16 @@
     return jnp.concatenate([high, low], axis=1)
 
 
+def twice(both):
+    return jnp.concatenate([both, both], axis=0)
+
+
 def right_of(x):
-    high, low = split(x)
-    both = jnp.concatenate([high, low], axis=1)
-    return jnp.concatenate([both, both], axis=0)
+    return twice(left_of(x))
+
+
+def joined(both):
+    return both[:, :N].astype(F32) + both[:, N:].astype(F32)
 
 
 def halves(product):
@@ -46,7 +52,7 @@
     return lax.dot_general(a, b, (((1,), (1,)), ((), ())), preferred_element_type=F32)
 
 
-def fill_tables(masks, tri, picks):
+def fill_tables(masks, levels, tri, picks):
     row = lax.broadcasted_iota(jnp.int32, (N, N), 0)
     col = lax.broadcasted_iota(jnp.int32, (N, N), 1)
     j, p, jj, pp = row // CH, row % CH, col // CH, col % CH
@@ -58,6 +64,7 @@
     sets.append((j == 3) & (jj < 3))
     for k, chosen in enumerate(sets):
         masks[k] = chosen.astype(F32)
+        levels[k] = jnp.concatenate([chosen.astype(F32).astype(BF)] * 2, axis=1)
     strict = steps & ((p > pp) | ((p == pp) & (j > jj)))
     masks[LEVELS + 1] = (strict | ((j == 3) & (jj < 3) & (p >= pp))).astype(F32)
     tri[...] = ((j == jj) & (pp <= p)).astype(F32)
@@ -92,8 +99,8 @@
     squares[...] = total if fresh else squares[...] + total
 
 
-def absorb(owners, fresh, half, weight, xs, acc):
-    cols = slice(half * 4 * N, (half + 1) * 4 * N)
+def absorb(owners, fresh, quarter, weight, xs, acc):
+    cols = slice(quarter * 2 * N, (quarter + 1) * 2 * N)
     kernel = jnp.concatenate(
         [weight[pl.ds(pl.multiple_of(o * 2 * N, 2 * N), 2 * N), cols] for o in owners], axis=0
     )
@@ -150,14 +157,18 @@
         )
         ratio = jnp.exp(jnp.where(causal, cc - cum_row[0:1, c * N : (c + 1) * N], -1e30))
         system = bb * ratio * gram
-        la[n] = system
+        la[n] = left_of(system)
         pairs = system * first
         scale = jnp.sum(pairs[CH : 2 * CH], axis=0, keepdims=True)
         third = system[2 * CH : 3 * CH] * masks[1, 2 * CH : 3 * CH, :]
         third = third - pltpu.roll(third, N - CH, 1) * scale
         start = eye - pairs
-        tt[n] = jnp.concatenate([start[: 2 * CH], start[2 * CH : 3 * CH] - third, start[3 * CH :]], axis=0)
-        tmp[n] = jnp.zeros((N, N), F32)
+        tt[n] = left_of(
+            jnp.concatenate(
+                [start[: 2 * CH], start[2 * CH : 3 * CH] - third, start[3 * CH :]], axis=0
+            )
+        )
+        tmp[n] = jnp.zeros((N, 2 * N), BF)
         xa, xb = bb * vv, bb * gg * kq
         ha, lo_a = split(xa)
         hb, lo_b = split(xb)
@@ -170,28 +181,28 @@
         et[n] = jnp.broadcast_to(jnp.exp(last), (8, N))
 
 
-def invert(ids, first, stop, masks, la, tt, tmp):
+def invert(ids, first, stop, levels, la, tt, tmp):
     top = 3 * CH
 
     def level(k, carry):
-        mask = masks[k, :top, :]
+        mask = levels[k, :top, :]
         for n in ids:
-            tmp[n, :top, :] = halves(dot(left_of(la[n, :top, :] * mask), right_of(tt[n])))
+            tmp[n, :top, :] = left_of(halves(dot(la[n, :top, :] * mask, twice(tt[n]))))
         for n in ids:
             t = tt[n, :top, :]
-            tt[n, :top, :] = t - halves(dot(left_of(t), right_of(tmp[n])))
+            tt[n, :top, :] = left_of(joined(t) - halves(dot(t, twice(tmp[n]))))
         return carry
 
     lax.fori_loop(first, stop, level, 0)
     if stop < LEVELS:
         return
     for n in ids:
-        tt[n, top:, :] = -halves(dot(left_of(la[n, top:, :]), right_of(tt[n])))
+        tt[n, top:, :] = left_of(-halves(dot(la[n, top:, :], twice(tt[n]))))
 
 
 def chunk_maps(n, tt, xh, xl, kt, eq, et, pq, rr, ov):
-    high, low = split(tt[n])
-    big = jnp.concatenate([high, low], axis=1)
+    big = tt[n]
+    high = big[:, :N]
     z = dot(big, jnp.concatenate([xh[n], xh[n]], axis=0)) + dot(high, xl[n])
     zh, zl = split(z)
     k = kt[n]
@@ -225,14 +236,15 @@
     m = seqs * NC
     return [
         pltpu.VMEM((LEVELS + 2, N, N), F32),
+        pltpu.VMEM((LEVELS + 1, N, 2 * N), BF),
         pltpu.VMEM((N, N), F32),
         pltpu.VMEM((N, NC * N), F32),
         pltpu.VMEM((seqs * N, 4 * N), BF),
         pltpu.VMEM((seqs * N, 8 * N), F32),
         pltpu.VMEM((seqs * N, N), F32),
-        pltpu.VMEM((m, N, N), F32),
-        pltpu.VMEM((m, N, N), F32),
-        pltpu.VMEM((m, N, N), F32),
+        pltpu.VMEM((m, N, 2 * N), BF),
+        pltpu.VMEM((m, N, 2 * N), BF),
+        pltpu.VMEM((m, N, 2 * N), BF),
         pltpu.VMEM((m, N, 2 * N), BF),
         pltpu.VMEM((m, N, 2 * N), BF),
         pltpu.VMEM((m, N, 2 * N), BF),
@@ -287,10 +299,14 @@
     return lax.rem(index + size, size)
 
 
+def sent(src, send_sem):
+    remote(src, src, send_sem, send_sem, **{C: lax.axis_index(C)}).wait_send()
+
+
 class Ring:
     def __init__(self, buf, sems, ny):
         self.buf, self.ny = buf, ny
-        self.s_right, self.r_right, self.s_left, self.r_left, self.s_pair, self.r_pair = sems
+        self.out, self.r_right, self.r_left, self.r_pair = sems
         self.y, self.c = lax.axis_index(Y), lax.axis_index(C)
         long, short = ny // 2, (ny - 1) // 2
         self.steps = [(long, short) if s % 2 == 0 else (short, long) for s in range(PARTS)]
@@ -303,28 +319,27 @@
     def owner(self, way, k):
         return wrap(self.y - (k + 1), self.ny) if way == 0 else wrap(self.y + (k + 1), self.ny)
 
-    def pair_index(self, way, k, s):
-        return (1 + k if way == 0 else 1 + self.steps[s][0] + k) * PARTS + s
-
     def hop(self, way, k, s):
         piece = self.piece(self.owner(way, k - 1), self.c, s)
         to = wrap(self.y + 1, self.ny) if way == 0 else wrap(self.y - 1, self.ny)
-        ss, rs = (self.s_right, self.r_right) if way == 0 else (self.s_left, self.r_left)
-        at = k * PARTS + s
-        return remote(piece, piece, ss.at[at], rs.at[at], **{Y: to})
+        arrival = (self.r_right, self.r_left)[way].at[k * PARTS + s]
+        send(piece, piece, self.out.at[0], arrival, **{Y: to})
+
+    def distance(self, way, k):
+        return (-(k + 1) if way == 0 else k + 1) % self.ny
 
     def to_pair(self, way, k, s):
         piece = self.piece(self.owner(way, k), self.c, s)
-        at = self.pair_index(way, k, s)
-        return remote(piece, piece, self.s_pair.at[at], self.r_pair.at[at], **{C: 1 - self.c})
+        arrival = self.r_pair.at[self.distance(way, k)]
+        send(piece, piece, self.out.at[1], arrival, **{C: 1 - self.c})
 
     def start(self):
         for s in range(PARTS):
             for way in range(2):
                 if self.steps[s][way] > 0:
-                    self.hop(way, 0, s).start()
+                    self.hop(way, 0, s)
         for s in range(PARTS):
-            self.to_pair(0, -1, s).start()
+            self.to_pair(0, -1, s)
 
     def forward(self, k, s):
         for way in range(2):
@@ -333,18 +348,16 @@
                 at = k * PARTS + s
                 arrived(self.piece(owner, self.c, s), (self.r_right, self.r_left)[way].at[at])
                 if k + 1 < self.steps[s][way]:
-                    self.hop(way, k + 1, s).start()
-                self.to_pair(way, k, s).start()
+                    self.hop(way, k + 1, s)
+                self.to_pair(way, k, s)
 
     def step(self, k):
         for s in range(PARTS):
             self.forward(k, s)
 
     def wait_pair(self, way, k):
-        for s in range(PARTS):
-            at = way if k < self.steps[s][way] else 1 - way
-            piece = self.piece(self.owner(at, k), 1 - self.c, s)
-            arrived(piece, self.r_pair.at[self.pair_index(at, k, s)])
+        block = self.buf.at[self.owner(way, k) * 2 + 1 - self.c]
+        arrived(block, self.r_pair.at[self.distance(way, k)])
 
     def owners(self, k):
         return [(0, k), (1, k)] if 2 * (k + 1) < self.ny else [(0, k)]
@@ -356,44 +369,17 @@
                 self.wait_pair(way, step)
 
     def drain(self):
-        for s in range(PARTS):
-            self.to_pair(0, -1, s).wait_send()
-            for way in range(2):
-                for k in range(self.steps[s][way]):
-                    self.hop(way, k, s).wait_send()
-                    self.to_pair(way, k, s).wait_send()
+        if self.ny > 1:
+            sent(self.buf.at[pl.ds(0, self.ny - 1)], self.out.at[0])
+        sent(self.buf.at[pl.ds(0, self.ny)], self.out.at[1])
 
 
 def exchange_head(buf, mine, sems, ny):
     y, c = lax.axis_index(Y), lax.axis_index(C)
-    sent = []
     order = sorted(range(1, 2 * ny), key=lambda k: -min(k // 2, ny - k // 2))
     for k in order:
         to = {Y: wrap(y + k // 2, ny), C: lax.rem(c + k % 2, 2)}
-        sent.append(send(buf.at[mine], buf.at[mine], sems[0].at[k - 1], sems[1].at[k - 1], **to))
-    return sent
-
-
-def await_head(buf, sems, ny):
-    y, c = lax.axis_index(Y), lax.axis_index(C)
-    for k in range(1, 2 * ny):
-        source = wrap(y - k // 2, ny) * 2 + lax.rem(c + k % 2, 2)
-        arrived(buf.at[source], sems[1].at[k - 1])
-
-
-def exchange_axis(axis, size, piece, sems):
-    me = lax.axis_index(axis)
-    order = sorted(range(1, size), key=lambda k: -min(k, size - k))
-    return [
-        send(piece(me), piece(me), sems[0].at[k - 1], sems[1].at[k - 1], **{axis: wrap(me + k, size)})
-        for k in order
-    ]
-
-
-def await_axis(axis, size, piece, sems):
-    me = lax.axis_index(axis)
-    for k in range(1, size):
-        arrived(piece(wrap(me - k, size)), sems[1].at[k - 1])
+        send(buf.at[mine], buf.at[mine], sems.at[0], sems.at[1], **to)
 
 
 def combine(buf, count):
@@ -409,12 +395,11 @@
 
 
 NAMES = (
-    "masks", "tri", "picks", "xs", "acc", "squares", "la", "tt", "tmp", "xh", "xl", "kt", "eq", "et", "pq",
-    "rr", "ov", "blocks", "nall", "weight", "cols", "vocab", "state", "blank", "lastn",
-    "lastm", "shaped", "hid", "part", "other", "sy", "sp", "tr1", "tr2", "tr3", "tr4",
-    "tr5", "tr6", "nr1", "nr2", "nr3", "nr4", "nr5", "nr6", "c1", "c2", "d1", "d2", "v1", "v2", "a1",
-    "a2", "b1", "b2", "z1", "z2", "x1", "x2", "p1", "p2", "g1", "g2", "h1", "h2",
-    "local", "free", "gain", "rates", "hgain", "fgain", "wanted", "length", "rate",
+    "masks", "levels", "tri", "picks", "xs", "acc", "squares", "la", "tt", "tmp", "xh", "xl",
+    "kt", "eq", "et", "pq", "rr", "ov", "blocks", "nall", "weight", "cols", "vocab", "state",
+    "blank", "lastn", "lastm", "shaped", "hid", "part", "other", "sy", "sp", "tr1", "tr2",
+    "tr3", "tr4", "nr1", "nr2", "nr3", "nr4", "c", "d", "v", "a", "b", "z", "x", "p", "g",
+    "h", "local", "free", "gain", "rates", "hgain", "fgain", "wanted", "length", "rate",
 )
 
 
@@ -479,12 +464,17 @@
     own.wait()
     pl.semaphore_wait(barrier, len(near))
 
-    ring = Ring(blocks, [r[f"tr{k}"] for k in range(1, 7)], ny)
+    ring = Ring(blocks, [r[f"tr{k}"] for k in range(1, 5)], ny)
     ring.start()
-    pair_vocab = []
+    last_sends = []
+
+    def shared(ref, sems):
+        arrived(ref, sems.at[1])
+        last_sends.append((ref, sems.at[0]))
+
     for q in range(4):
         src, dst = vocab_piece(1 - c, q)
-        pair_vocab.append(send(src, dst, r["v1"].at[q], r["v2"].at[q], **{C: 1 - c}))
+        send(src, dst, r["v"].at[0], r["v"].at[1], **{C: 1 - c})
 
     pending = []
     free = r["free"]
@@ -510,7 +500,7 @@
 
     if pending:
         plane_step()
-    fill_tables(r["masks"], r["tri"], r["picks"])
+    fill_tables(r["masks"], r["levels"], r["tri"], r["picks"])
     for copy in small:
         copy.wait()
     place_rates(rate_t, weight, r["blank"])
@@ -524,51 +514,49 @@
         widen(owners, fresh, blocks, gain, r["xs"], squares_of)
         return owners, fresh
 
-    def take(owners, fresh, half):
-        absorb(owners, fresh, half, weight, r["xs"], acc)
+    def take(owners, fresh, quarters):
+        for quarter in quarters:
+            absorb(owners, fresh, quarter, weight, r["xs"], acc)
 
     for k in range(ring.last + 1):
-        half = PARTS // 2
-        for s in range(half):
-            ring.forward(k, s)
-        found = ready([(0, -1)] if k == 0 else ring.owners(k - 1))
-        take(*found, 0)
-        for s in range(half, PARTS):
-            ring.forward(k, s)
-        take(*found, 1)
+        ring.forward(k, 0)
+        if k:
+            found = ready([(0, -1)] if k == 1 else ring.owners(k - 2))
+        ring.forward(k, 1)
+        if k:
+            take(*found, (0,))
         plane_next()
-
-    col_sent = []
+        ring.forward(k, 2)
+        if k:
+            take(*found, (1,))
+        ring.forward(k, 3)
+        if k:
+            take(*found, (2, 3))
+        plane_next()
+
     for k in range(1, heads):
         py, pc = wrap(y + k // 2, ny), lax.rem(c + k % 2, 2)
         to = pl.multiple_of((py * 2 + pc) * N, N)
-        col_sent.append(
-            send(out_weight.at[rows_here, pl.ds(to, N)], cols.at[me, rows_here, :],
-                 r["c1"].at[k - 1], r["c2"].at[k - 1], **{Y: py, C: pc})
-        )
-    found = ready(ring.owners(ring.last))
-    take(*found, 0)
-    take(*found, 1)
+        send(out_weight.at[rows_here, pl.ds(to, N)], cols.at[me, rows_here, :], r["c"].at[0],
+             r["c"].at[1], **{Y: py, C: pc})
+    for k in range(max(ring.last - 1, 0), ring.last + 1):
+        take(*ready(ring.owners(k)), range(4))
+    plane_next()
     for s in range(SEQS):
-        plane_next()
         sequence_inputs(
-            s, lengths[s], rate[0], heads, acc, squares_of, r["masks"], r["tri"], r["picks"],
+            s, lengths[s], rate[0, 0], heads, acc, squares_of, r["masks"], r["tri"], r["picks"],
             r["la"], r["tt"], r["tmp"], r["xh"], r["xl"], r["kt"], r["eq"], r["et"],
         )
     plane_next()
     ids = range(SEQS * NC)
-    invert(ids, 2, 5, r["masks"], r["la"], r["tt"], r["tmp"])
+    invert(ids, 2, 5, r["levels"], r["la"], r["tt"], r["tmp"])
     plane_next()
     own_cols.wait()
-    for k in range(1, heads):
-        source = wrap(y - k // 2, ny) * 2 + lax.rem(c + k % 2, 2)
-        arrived(cols.at[source, rows_here, :], r["c2"].at[k - 1])
+    shared(cols.at[pl.ds(0, heads - 1), rows_here, :], r["c"])
     bands = cols.at[:, rows_here, :]
     for dx in range(1, nx):
-        col_sent.append(
-            send(bands, bands, r["d1"].at[dx - 1], r["d2"].at[dx - 1], **{X: wrap(x + dx, nx)})
-        )
-    invert(ids, 5, LEVELS, r["masks"], r["la"], r["tt"], r["tmp"])
+        send(bands, bands, r["d"].at[0], r["d"].at[1], **{X: wrap(x + dx, nx)})
+    invert(ids, 5, LEVELS, r["levels"], r["la"], r["tt"], r["tmp"])
     plane_next()
     for n in ids:
         chunk_maps(
@@ -592,17 +580,16 @@
 
     lastn, lastm = r["lastn"], r["lastm"]
     lastn[me] = last_rows(nall)
-    sends = exchange_head(lastn, me, (r["a1"], r["a2"]), ny)
-    bulk = Ring(nall, [r[f"nr{k}"] for k in range(1, 7)], ny)
+    exchange_head(lastn, me, r["a"], ny)
+    bulk = Ring(nall, [r[f"nr{k}"] for k in range(1, 5)], ny)
     residual = last_rows(blocks)
-    for dx in range(1, nx):
-        theirs = pl.ds(pl.multiple_of(wrap(x - dx, nx) * band, band), band)
-        arrived(cols.at[:, theirs, :], r["d2"].at[dx - 1])
-    await_head(lastn, (r["a1"], r["a2"]), ny)
+    if nx > 1:
+        shared(cols.at[:, pl.ds(0, (nx - 1) * band), :], r["d"])
+    shared(lastn.at[pl.ds(0, heads - 1)], r["a"])
     wide = jnp.concatenate([lastn[b].astype(BF) for b in range(heads)], axis=1)
     every_col = jnp.concatenate([cols[b] for b in range(heads)], axis=0)
     lastm[me] = (residual + dot(wide, every_col)).astype(BF).astype(F32)
-    sends += exchange_head(lastm, me, (r["b1"], r["b2"]), ny)
+    exchange_head(lastm, me, r["b"], ny)
     bulk.start()
     late = list(range(ring.last + 1))
 
@@ -612,7 +599,7 @@
 
     while pending:
         plane_step()
-    await_head(lastm, (r["b1"], r["b2"]), ny)
+    shared(lastm.at[pl.ds(0, heads - 1)], r["b"])
     squares = sum(lastm[b] * lastm[b] for b in range(heads))
     factor = lax.rsqrt(jnp.sum(squares, axis=1, keepdims=True) / (heads * N) + ROW_EPSILON)
     per = heads // 8
@@ -628,27 +615,22 @@
     def cell(px, pz):
         return hid.at[px * nz + pz]
 
-    def to_row(pz, k):
+    def to_row(pz):
         for dx in range(1, nx):
-            at = (dx - 1) * nz + k
-            sends.append(
-                send(cell(x, pz), cell(x, pz), r["x1"].at[at], r["x2"].at[at], **{X: wrap(x + dx, nx)})
-            )
-
-    sends += exchange_axis(Z, nz, lambda pz: cell(x, pz), (r["z1"], r["z2"]))
-    to_row(z, 0)
+            send(cell(x, pz), cell(x, pz), r["x"].at[0], r["x"].at[1], **{X: wrap(x + dx, nx)})
+
+    for k in sorted(range(1, nz), key=lambda k: -min(k, nz - k)):
+        send(cell(x, z), cell(x, z), r["z"].at[0], r["z"].at[k], **{Z: wrap(z + k, nz)})
+    to_row(z)
     bulk_step()
     for k in sorted(range(1, nz), key=lambda k: min(k, nz - k)):
         pz = wrap(z - k, nz)
-        arrived(cell(x, pz), r["z2"].at[k - 1])
-        to_row(pz, k)
+        arrived(cell(x, pz), r["z"].at[k])
+        to_row(pz)
     bulk_step()
     for q in range(4):
         vocab_copies[q].wait()
-        rows = pl.ds(
-            pl.multiple_of(q * 2 * VOCAB_HERE + (1 - c) * VOCAB_HERE, VOCAB_HERE), VOCAB_HERE
-        )
-        arrived(r["vocab"].at[rows, :], r["v2"].at[q])
+    shared(r["vocab"].at[pl.ds(0, 4 * VOCAB_HERE), :], r["v"])
     lane = lax.broadcasted_iota(jnp.int32, (N, N), 1)
     rank = lax.broadcasted_iota(jnp.int32, (N, N), 0)
     source = ((lane // 4) % 4) * 8 + lane // 16
@@ -657,9 +639,10 @@
     wanted = jnp.broadcast_to(next_token[...].astype(F32), (8, N))
     wanted = jnp.dot(wanted, permute, precision=HI, preferred_element_type=F32)[0:1]
     wanted = (wanted + 0.5).astype(jnp.int32)
-    for dx in range(1, nx):
-        for k in range(nz):
-            arrived(cell(wrap(x - dx, nx), wrap(z - k, nz)), r["x2"].at[(dx - 1) * nz + k])
+    if nx > 1:
+        shared(hid.at[pl.ds(0, (nx - 1) * nz)], r["x"])
+    if nz > 1:
+        last_sends.append((hid.at[pl.ds(0, nz - 1)], r["z"].at[0]))
 
     everyone = jnp.concatenate([hid[k] for k in range(SOURCES)], axis=0)
     product = dot_nt(r["vocab"][...], everyone)
@@ -679,8 +662,8 @@
     part, other = r["part"], r["other"]
     part[0] = packed[:VOCAB_HERE]
     part[1] = packed[VOCAB_HERE:]
-    sends.append(send(part.at[1 - c], other, r["p1"].at[0], r["p2"].at[0], **{C: 1 - c}))
-    arrived(other, r["p2"].at[0])
+    send(part.at[1 - c], other, r["p"].at[0], r["p"].at[1], **{C: 1 - c})
+    shared(other, r["p"])
     logits = part[c] + other[...]
     vocab_ids = (((z * nx + x) * ny + y) * 2 + c) * VOCAB_HERE + rank[:VOCAB_HERE]
     top = jnp.max(logits, axis=0, keepdims=True)
@@ -688,9 +671,9 @@
     target = jnp.sum(jnp.where(vocab_ids == wanted, logits, 0.0), axis=0, keepdims=True)
     sy, sp = r["sy"], r["sp"]
     put_stats(sy, me, top, total, target)
-    sends += exchange_head(sy, me, (r["g1"], r["g2"]), ny)
+    exchange_head(sy, me, r["g"], ny)
     bulk_step()
-    await_head(sy, (r["g1"], r["g2"]), ny)
+    shared(sy.at[pl.ds(0, heads - 1)], r["g"])
     put_stats(sp, slot, *combine(sy, heads))
     far = sorted(
         (k for k in range(1, nz * nx)),
@@ -698,7 +681,7 @@
     )
     for k in far:
         to = {Z: wrap(z + k % nz, nz), X: wrap(x + k // nz, nx)}
-        sends.append(send(sp.at[slot], sp.at[slot], r["h1"].at[k - 1], r["h2"].at[k - 1], **to))
+        send(sp.at[slot], sp.at[slot], r["h"].at[0], r["h"].at[1], **to)
     while late:
         bulk_step()
     bulk.wait_all_pairs()
@@ -713,17 +696,17 @@
     lax.fori_loop(0, SEQS, mix, 0)
     ring.drain()
     bulk.drain()
-    for copy in col_sent + pair_vocab:
-        copy.wait_send()
-    for k in range(1, nz * nx):
-        arrived(sp.at[wrap(x - k // nz, nx) * nz + wrap(z - k % nz, nz)], r["h2"].at[k - 1])
+    for src, sem in last_sends:
+        sent(src, sem)
+    last_sends.clear()
+    shared(sp.at[pl.ds(0, nz * nx - 1)], r["h"])
     top, total, target = combine(sp, nz * nx)
     result = jnp.broadcast_to(target - (top + jnp.log(total)), (8, N))
     likelihood[...] = lax.dot_general(
         result, permute, (((1,), (1,)), ((), ())), precision=HI, preferred_element_type=F32
     )[0:1]
-    for copy in sends:
-        copy.wait_send()
+    for src, sem in last_sends:
+        sent(src, sem)
 
 
 def deliver_kernel(*refs):
@@ -754,7 +737,6 @@
     vmem = pl.BlockSpec(memory_space=pltpu.VMEM)
     hbm = pl.BlockSpec(memory_space=pltpu.HBM)
     dma = lambda n: pltpu.SemaphoreType.DMA((max(n, 1),))
-    group = 2 * ny - 1
     scratch = mixer_scratch(SEQS, heads, mix_weight.shape[1]) + [
         pltpu.VMEM((heads, rows, N), BF),
         pltpu.VMEM((heads, rows, N), BF),
@@ -773,11 +755,8 @@
         pltpu.VMEM((nz * nx, 4, N), F32),
     ]
     hops = PARTS * max(ny // 2, 1)
-    scratch += [dma(hops)] * 4 + [dma(PARTS * ny)] * 2
-    scratch += [dma(hops)] * 4 + [dma(PARTS * ny)] * 2
-    scratch += [dma(group)] * 2 + [dma(nx - 1)] * 2 + [dma(4)] * 2 + [dma(group)] * 4
-    scratch += [dma(nz - 1)] * 2 + [dma((nx - 1) * nz)] * 2 + [dma(1)] * 2
-    scratch += [dma(group)] * 2 + [dma(nz * nx - 1)] * 2
+    scratch += [dma(2), dma(hops), dma(hops), dma(ny)] * 2
+    scratch += [dma(2)] * 5 + [dma(nz)] + [dma(2)] * 4
     scratch += [dma(15), pltpu.SemaphoreType.REGULAR((2,))]
     scratch += [
         pltpu.VMEM((heads, N), F32),
@@ -786,7 +765,7 @@
         pltpu.VMEM((heads, N), F32),
         pltpu.VMEM((1, N), jnp.int32),
         pltpu.SMEM((SEQS,), jnp.int32),
-        pltpu.SMEM((1,), F32),
+        pltpu.SMEM((1, 1), F32),
     ]
     wanted = next_token.reshape(1, everyone)
     if everyone < N:
@@ -811,7 +790,7 @@
         norm_gain.reshape(heads, N),
         mix_weight,
         rate_weight.T,
-        decay_rate,
+        decay_rate.reshape(1, 1),
         head_gain.reshape(1, N),
         out_weight,
         final_gain.reshape(heads, N),

time: 80.3 us -> 75.5 us (0.940)
  Pallas kernels: 78.7 us -> 74.1 us
    pallas_call x1, Pallas kernels: 77 us -> 72.3 us  [on_device(): pl.pallas_call(functools.partial(one_kernel, sizes), out_shape=(jax.Shape...]
where the time goes in v3:
time: 75.5 us; the launch traced here: 75.4 us
  Pallas kernels  74.1 us (98%)
  between operations  1.29 us (2%)
    pallas_call x1, Pallas kernels, on_device(): pl.pallas_call(functools.partial(one_kernel, sizes), out_shape=(jax.Shape...  72.3 us
    pallas_call x1, Pallas kernels, deliver(): pl.pallas_call(deliver_kernel, out_shape=tuple((jax.ShapeDtypeStruct(a.sh...  1.76 us

profile of v3, /device:TPU:1, one launch (start us, length us, event | category | flops | bytes accessed | tf_op | source)
XLA Modules:
  0.0 75.4 jit_solution(16183290608404152686)
XLA Ops:
  1.3 72.3 %shard_map.139 = (bf16[512,128]{1,0:T(8,128)(2,1)}, f32[4,128,128]{2,1,0:T(8,128)}, f32[1,128]{1,0:T(1,128)}) custom-call(bf16[512,128]{1,0:T(8,128)(2,1)} %refs_0_.1, s32[4]{0:T(128)} %refs_1_.1, f32[4,128,128]{2,1,0:T(8,128)} %bitcast.12, f32[16,128]{1,0:T(8,128)} %bitcast.14, bf16[2048,896]{1,0:T(8,128)(2,1)} %refs_4_.1, bf16[4,2048]{1,0:T(4,128)(2,1)} %bitcast.13, ...), custom_call_target="tpu_custom_call" | custom-call | tf_op jit(solution)/shard_map/pallas_call | solution.py:773
  73.6 1.8 %shard_map.140 = (bf16[512,128]{1,0:T(8,128)(2,1)}, f32[4,128,128]{2,1,0:T(8,128)}, f32[1,128]{1,0:T(1,128)}) custom-call(bf16[512,128]{1,0:T(8,128)(2,1)} %get-tuple-element.9.refs_0_, f32[4,128,128]{2,1,0:T(8,128)} %get-tuple-element.10.refs_1_, f32[1,128]{1,0:T(1,128)} %get-tuple-element.11.refs_2_), custom_call_target="tpu_custom_call" | custom-call | tf_op jit(solution)/shard_map/pallas_call | solution.py:722
